TPU v7x, 128 devices: a whole 4x4x4 slice. The times are simulated.
128 devices in a mesh: row: 8 (over y, z_hi), col: 16 (over z_lo, x, core).
Axes of the slice: x: 4, y: 4, z: 4 (z_hi: 2, z_lo: 2; z = z_hi * 2 + z_lo), core: 2. Of those that a mesh axis runs over, the one named last changes fastest.
Arguments:
- inverse: float32 [24576, 24576], P('row', 'col'), may hold values from -0.0546875 to 0.0546875
- parent_panel: float32 [24576, 256], P(('row', 'col')), may hold values from -1.8 to 1.8
- child_panel: float32 [24576, 256], P(('row', 'col')), may hold values from -1.8 to 1.8
- child_top: float32 [256, 256], replicated, may hold values from -0.375 to 0.375
- diag_parent: float32 [256, 256], replicated, may hold values from -12 to 12
- diag_child: float32 [256, 256], replicated, may hold values from -12 to 12
- parent_blocks: int32 [192], replicated, may hold values from 0 to 1
- child_blocks: int32 [192], replicated, may hold values from 0 to 1, as said below
Outputs:
- parent_column: float32 [24576, 256], P(('row', 'col'))
- parent_diagonal: float32 [256, 256], replicated
- child_column: float32 [24576, 256], P(('row', 'col'))
- child_upper: float32 [256, 256], replicated
- child_diagonal: float32 [256, 256], replicated
Inputs may be any that keep to these rules, and one draw needn't show every extreme that they name: `child_blocks`: each entry is 0 or 1, and is 1 only where parent_blocks is 1.
All inputs are finite; a program needn't handle non-finite values.
Results may differ from a plain program's by a relative error of at most 0.000086.
Values sent between devices are 32-bit elements; how exact they have to be, the bound alone decides.
No kernel may reach another device: no remote copies, remote signals or barrier semaphores. Data moves between devices by JAX's collectives and lax.ppermute only.
A program may use at most 128 MiB of HBM per device.

v0:
```python
import jax.numpy as jnp
from jax import lax

BLK = 128


def expand_mask(blocks):
    flags = jnp.repeat(blocks, BLK, total_repeat_length=blocks.shape[0] * BLK)
    return flags.astype(jnp.float32)[:, None]


def matmul(left, right):
    return jnp.dot(left, right, precision=lax.Precision.HIGHEST, preferred_element_type=jnp.float32)


def reference(
    inverse,
    parent_panel,
    child_panel,
    child_top,
    diag_parent,
    diag_child,
    parent_blocks,
    child_blocks,
):
    parent_mask = expand_mask(parent_blocks)
    child_mask = expand_mask(child_blocks)
    parent_masked = parent_panel * parent_mask
    child_masked = child_panel * child_mask
    parent_image = matmul(inverse, parent_masked)
    child_image = matmul(inverse, child_masked)
    parent_column = -(parent_mask * parent_image)
    parent_diagonal = diag_parent - matmul(parent_masked.T, parent_column)
    child_column = -(child_mask * (matmul(parent_column, child_top) + child_image))
    child_upper = -(matmul(parent_diagonal, child_top) + matmul(parent_column.T, child_masked))
    child_diagonal = (
        diag_child - matmul(child_top.T, child_upper) - matmul(child_masked.T, child_column)
    )
    return (parent_column, parent_diagonal, child_column, child_upper, child_diagonal)


def solution(mesh):
    return reference
```

profile of v0, /device:TPU:1, one launch (start us, length us, event | category | flops | bytes accessed | tf_op | source)
XLA Modules:
  0.0 557.0 jit_solution(16473051443677480515)
XLA Ops:
  7.2 1.3 dynamic-slice.9
  8.5 0.7 add_bitcast_fusion.1
  9.3 0.6 fusion.15
  9.9 1.6 scatter_custom_fusion
  12.0 1.3 collective-permute-start
  13.3 0.7 collective-permute-start.1
  14.0 1.2 dynamic-slice.39
  15.2 1.9 dynamic-slice.13
  17.1 2.0 dynamic-slice.17
  19.1 2.0 dynamic-slice.18
  21.0 1.9 dynamic-slice.15
  22.9 1.2 dynamic-slice.25
  24.1 1.3 dynamic-slice.24
  26.7 1.9 dynamic-slice.40
  30.5 1.9 dynamic-slice.41
  33.0 1.9 dynamic-slice.42
  35.6 1.3 fusion.20
  39.0 2.1 fusion.18
  41.1 20.8 %all-reduce.6 = s32[128]{0:T(128)S(1)} all-reduce(s32[128]{0:T(128)S(1)} %fusion.18), channel_id=21, replica_groups=mesh['axis_0'=2,'axis_1'=32,'axis_2'=2] {'axis_1'}, use_global_device_ids=true, to_apply=%add.6 | all-reduce | flops 128 | bytes 1024
  62.3 0.6 slice.42
  62.9 1.3 collective-permute-start.2
  64.1 7.3 %collective-permute-done.2 = s32[1,1]{1,0:T(1,128)} collective-permute-done((s32[1,1]{1,0:T(1,128)}, s32[1,1]{1,0:T(1,128)}, u32[]{:S(2)}, u32[]{:S(2)}) %collective-permute-start.2) | collective-permute-done | bytes 36 | tf_op slice.29
  71.5 4.4 collective-permute-start.3
  76.0 1.2 pad_add_fusion
  77.2 0.6 dynamic-slice_select_fusion
  78.4 5.8 %collective-permute-start.4 = (s32[1,1]{1,0:T(1,128)}, s32[1,1]{1,0:T(1,128)}, u32[]{:S(2)}, u32[]{:S(2)}) collective-permute-start(s32[1,1]{1,0:T(1,128)} %get-tuple-element.36), channel_id=6, source_target_pairs={{0,64},{1,65},{2,66},{3,67},{4,68},{5,69},{6,70},{7,71},{8,72},{9,... | collective-permute-start | bytes 20 | tf_op slice.33
  84.5 1.3 pad_add_fusion.1
  86.3 8.5 %all-reduce = s32[1]{0:T(128)} all-reduce(s32[1]{0:T(128)} %bitcast.14), channel_id=7, replica_groups={{0,2,4,6,8,10,12,14,16,18,20,22,24,26,28,30,32,34,36,38,40,42,44,46,48,..., use_global_device_ids=true, to_apply=%add.clone | all-reduce | flops 1 | bytes 8 | tf_op reshape.54
  94.8 0.6 fusion.37
  95.4 0.7 broadcast_add_fusion
  96.7 2.7 collective-permute-start.5
  99.4 1.2 collective-permute-start.6
  100.6 0.6 collective-permute-start.7
  101.3 1.3 broadcast_select_fusion.1
  102.7 0.7 dynamic-slice.43
  103.5 0.6 slice.49
  104.0 3.2 collective-permute-start.8
  107.5 0.7 pad_add_fusion.4
  108.4 2.0 gather_fusion
  110.4 2.0 gather_fusion.1
  112.5 1.0 broadcast_multiply_fusion.1
  113.5 28.5 %collective-permute-start.9 = (f32[192,256]{1,0:T(8,128)S(1)}, f32[192,256]{1,0:T(8,128)S(1)}, u32[]{:S(2)}, u32[]{:S(2)}) collective-permute-start(f32[192,256]{1,0:T(8,128)S(1)} %broadcast_multiply_fusion.1), channel_id=12, source_target_pairs={{0,0},{1,16},{2,32},{3,48},{4,64},{5,80},{6,96},{7,112},{8,1},{9,1... | collective-permute-start | bytes 589832 | tf_op jit(solution)/mul | solution.py:28
  142.0 2.6 collective-permute-done.9
  144.6 0.7 copy-done.8
  145.3 1.0 broadcast_multiply_fusion
  146.3 5.9 %collective-permute-start.10 = (f32[192,256]{1,0:T(8,128)S(1)}, f32[192,256]{1,0:T(8,128)S(1)}, u32[]{:S(2)}, u32[]{:S(2)}) collective-permute-start(f32[192,256]{1,0:T(8,128)S(1)} %broadcast_multiply_fusion), channel_id=16, source_target_pairs={{0,0},{1,16},{2,32},{3,48},{4,64},{5,80},{6,96},{7,112},{8,1},{9,1... | collective-permute-start | bytes 589832 | tf_op jit(solution)/mul | solution.py:29
  152.2 6.8 %collective-permute-done.10 = f32[192,256]{1,0:T(8,128)S(1)} collective-permute-done((f32[192,256]{1,0:T(8,128)S(1)}, f32[192,256]{1,0:T(8,128)S(1)}, u32[]{:S(2)}, u32[]{:S(2)}) %collective-permute-start.10) | collective-permute-done | bytes 196640 | tf_op jit(solution)/mul | solution.py:29
  159.0 0.7 copy-done.9
  159.8 43.4 %all-gather.7.cloned.1.call-done = f32[1536,256]{1,0:T(8,128)} async-done(((f32[192,256]{1,0:T(8,128)}), f32[1536,256]{1,0:T(8,128)}) %all-gather.7.cloned.1.call-update) | async-done | bytes 1572880 | tf_op jit(solution)/mul | solution.py:28
  203.2 19.4 %fusion.22 = f32[256,3072]{0,1:T(8,128)} fusion(f32[1536,256]{1,0:T(8,128)} %all-gather.7.cloned.1.call-done, f32[3072,1536]{1,0:T(8,128)} %param.8), kind=kOutput, calls=%fused_computation.58 | convolution fusion | flops 14495514624 | bytes 23592960 | tf_op jit(solution)/dot_general | solution.py:13
  222.9 32.9 %all-gather.9.cloned.1.call-done = f32[1536,256]{1,0:T(8,128)} async-done(((f32[192,256]{1,0:T(8,128)}), f32[1536,256]{1,0:T(8,128)}) %all-gather.9.cloned.1.call-update) | async-done | bytes 1572880 | tf_op jit(solution)/mul | solution.py:29
  255.8 19.4 %fusion.23 = f32[256,3072]{0,1:T(8,128)} fusion(f32[1536,256]{1,0:T(8,128)} %all-gather.9.cloned.1.call-done, f32[3072,1536]{1,0:T(8,128)} %param.8), kind=kOutput, calls=%fused_computation.59 | convolution fusion | flops 14495514624 | bytes 23592960 | tf_op jit(solution)/dot_general | solution.py:13
  275.3 45.2 %reduce-scatter.7.cloned.1.call-done = f32[256,192]{0,1:T(8,128)} async-done(((f32[256,3072]{0,1:T(8,128)}), f32[256,192]{0,1:T(8,128)}) %reduce-scatter.7.cloned.1.call-update) | async-done | bytes 196624
  320.5 66.7 %reduce-scatter.9.cloned.1.call-done = f32[256,192]{0,1:T(8,128)} async-done(((f32[256,3072]{0,1:T(8,128)}), f32[256,192]{0,1:T(8,128)}) %reduce-scatter.9.cloned.1.call-update) | async-done | bytes 196624
  387.2 1.4 fusion.4
  388.6 1.4 fusion.24
  390.0 2.4 fusion.7
  392.4 2.4 fusion.6
  394.9 0.8 fusion.8
  395.7 149.8 %all-reduce.10.cloned.1.call-done = (f32[256,256]{1,0:T(8,128)}, f32[256,256]{1,0:T(8,128)}, f32[256,256]{0,1:T(8,128)}) async-done(((f32[256,256]{1,0:T(8,128)}, f32[256,256]{1,0:T(8,128)}, f32[256,256]{0,1:T(8,128)}), (f32[256,256]{1,0:T(8,128)}, f32[256,256]{1,0:T(8,128)}, f32[256,256]{0,1:T(8,128)})) %all-reduce.10.cloned.1.call-update) | async-done | bytes 786448 | tf_op jit(solution)/dot_general | solution.py:13
  545.5 1.0 sub.19
  546.5 1.4 fusion.2
  548.0 1.6 fusion.1
  549.6 0.8 copy.8
  (57 shorter events, 4.4 us)
Async XLA Ops:
  7.2 380.1 %copy-start = (f32[256,256]{1,0:T(8,128)S(1)}, f32[256,256]{1,0:T(8,128)}, u32[]{:S(2)}) copy-start(f32[256,256]{1,0:T(8,128)} %param.11) | copy-start | bytes 786436
  7.2 196.0 %all-gather.7.cloned.1.call-start = ((), (), s32[]{:S(2)}) async-start(), calls=%async_computation.2 | async-start | bytes 1769472 | tf_op jit(solution)/mul | solution.py:28
  12.0 26.9 %collective-permute-start = (s32[3]{0:T(128)S(1)}, s32[3]{0:T(128)S(1)}, u32[]{:S(2)}, u32[]{:S(2)}) collective-permute-start(s32[3]{0:T(128)S(1)} %slice_reduce_fusion), channel_id=1, source_target_pairs={{2,0},{4,2},{6,4},{8,6},{10,8},{12,10},{16,12},{18,14},{20,16},{24... | collective-permute-start | bytes 44 | tf_op reshape.32
  13.3 25.6 %collective-permute-start.1 = (s32[3]{0:T(128)S(1)}, s32[3]{0:T(128)S(1)}, u32[]{:S(2)}, u32[]{:S(2)}) collective-permute-start(s32[3]{0:T(128)S(1)} %slice_reduce_fusion), channel_id=2, source_target_pairs={{10,6},{12,8},{14,10},{18,12},{20,14},{22,16},{26,18},{28,20},{30,... | collective-permute-start | bytes 44 | tf_op reshape.32
  62.9 8.6 %collective-permute-start.2 = (s32[1,1]{1,0:T(1,128)}, s32[1,1]{1,0:T(1,128)}, u32[]{:S(2)}, u32[]{:S(2)}) collective-permute-start(s32[1,1]{1,0:T(1,128)} %slice.42), channel_id=4, source_target_pairs={{62,0},{63,1},{126,64},{127,65}} | collective-permute-start | bytes 20 | tf_op slice.29
  71.5 4.5 collective-permute-start.3
  78.4 6.0 %collective-permute-start.4 = (s32[1,1]{1,0:T(1,128)}, s32[1,1]{1,0:T(1,128)}, u32[]{:S(2)}, u32[]{:S(2)}) collective-permute-start(s32[1,1]{1,0:T(1,128)} %get-tuple-element.36), channel_id=6, source_target_pairs={{0,64},{1,65},{2,66},{3,67},{4,68},{5,69},{6,70},{7,71},{8,72},{9,... | collective-permute-start | bytes 20 | tf_op slice.33
  96.7 4.7 collective-permute-start.5
  99.4 1.9 collective-permute-start.6
  100.6 0.7 collective-permute-start.7
  104.0 3.5 collective-permute-start.8
  113.5 31.1 %collective-permute-start.9 = (f32[192,256]{1,0:T(8,128)S(1)}, f32[192,256]{1,0:T(8,128)S(1)}, u32[]{:S(2)}, u32[]{:S(2)}) collective-permute-start(f32[192,256]{1,0:T(8,128)S(1)} %broadcast_multiply_fusion.1), channel_id=12, source_target_pairs={{0,0},{1,16},{2,32},{3,48},{4,64},{5,80},{6,96},{7,112},{8,1},{9,1... | collective-permute-start | bytes 589832 | tf_op jit(solution)/mul | solution.py:28
  144.6 0.7 copy-start.8
  145.3 110.5 %all-gather.9.cloned.1.call-start = ((), (), s32[]{:S(2)}) async-start(), calls=%async_computation.3 | async-start | bytes 1769472 | tf_op jit(solution)/mul | solution.py:29
  146.3 12.7 %collective-permute-start.10 = (f32[192,256]{1,0:T(8,128)S(1)}, f32[192,256]{1,0:T(8,128)S(1)}, u32[]{:S(2)}, u32[]{:S(2)}) collective-permute-start(f32[192,256]{1,0:T(8,128)S(1)} %broadcast_multiply_fusion), channel_id=16, source_target_pairs={{0,0},{1,16},{2,32},{3,48},{4,64},{5,80},{6,96},{7,112},{8,1},{9,1... | collective-permute-start | bytes 589832 | tf_op jit(solution)/mul | solution.py:29
  159.0 0.7 copy-start.9
  159.7 160.8 %reduce-scatter.7.cloned.1.call-start = ((), (), s32[]{:S(2)}) async-start(), calls=%async_computation.4 | async-start | bytes 3342336
  222.6 164.6 %reduce-scatter.9.cloned.1.call-start = ((), (), s32[]{:S(2)}) async-start(), calls=%async_computation.5 | async-start | bytes 3342336
  275.2 117.2 %copy-start.4 = (f32[192,256]{1,0:T(8,128)S(1)}, f32[192,256]{1,0:T(8,128)}, u32[]{:S(2)}) copy-start(f32[192,256]{1,0:T(8,128)} %param.7) | copy-start | bytes 589828
  275.2 119.6 %copy-start.7 = (f32[256,256]{1,0:T(8,128)S(1)}, f32[256,256]{1,0:T(8,128)}, u32[]{:S(2)}) copy-start(f32[256,256]{1,0:T(8,128)} %param.13) | copy-start | bytes 786436
  275.2 270.3 %copy-start.6 = (f32[256,256]{1,0:T(8,128)S(1)}, f32[256,256]{1,0:T(8,128)}, u32[]{:S(2)}) copy-start(f32[256,256]{1,0:T(8,128)} %param.9) | copy-start | bytes 786436
  275.2 270.3 %all-reduce.10.cloned.1.call-start = ((), (), s32[]{:S(2)}) async-start(), calls=%async_computation.6 | async-start | bytes 1572864 | tf_op jit(solution)/dot_general | solution.py:13
  320.5 74.4 %copy-start.1 = (f32[256,192]{0,1:T(8,128)S(1)}, f32[256,192]{0,1:T(8,128)}, u32[]{:S(2)}) copy-start(f32[256,192]{0,1:T(8,128)} %reduce-scatter.7.cloned.1.call-done) | copy-start | bytes 589828
  388.6 161.0 %copy-start.5 = (f32[192,256]{1,0:T(8,128)}, f32[192,256]{1,0:T(8,128)S(1)}, u32[]{:S(2)}) copy-start(f32[192,256]{1,0:T(8,128)S(1)} %fusion.4) | copy-start | bytes 589828
  546.5 4.0 copy-start.2
  548.0 2.5 copy-start.3
Sparse Core Ops, SparseCore 0:
  145.4 57.7 all-gather.6
  206.1 49.6 all-gather.8
  258.2 62.2 reduce-scatter.6
  322.8 64.4 reduce-scatter.8
  394.9 150.5 all-reduce.9
where the time goes:
time: 558 us; the launch traced here: 557 us
  waiting for transfers between devices  356 us (64%)
  starting transfers between devices  55.9 us (10%)
  matrix products  49.4 us (9%)
  local copies, waits for them, and re-layouts  29.3 us (5%)
  blocking collectives  29.3 us (5%)
  between operations  20.5 us (4%)
  other arithmetic  16.9 us (3%)
    dot_general x1, waiting for transfers between devices, matmul(): jnp.dot(left, right, precision=lax.Precision.HIGHEST, preferred_element_t...  150 us
    unnamed x16, waiting for transfers between devices  120 us
    dot_general x8, matrix products, matmul(): jnp.dot(left, right, precision=lax.Precision.HIGHEST, preferred_element_t...  49.4 us
    mul x2, waiting for transfers between devices, reference(): parent_masked = parent_panel * parent_mask  46 us
    mul x2, waiting for transfers between devices, reference(): child_masked = child_panel * child_mask  39.7 us
    unnamed x2, blocking collectives  29.3 us
    mul x2, starting transfers between devices, reference(): parent_masked = parent_panel * parent_mask  28.5 us
    unnamed x42, local copies, waits for them, and re-layouts  24.1 us
  transfers between devices with their start and end apart: 16, of which 11 were waited for; matrix products, arithmetic and copies ran while one was open for 11% of the time, Pallas kernels for 0%

commit v1 on v0

v1 whole, which is shorter than its diff:
```python
import jax
import jax.numpy as jnp
from jax import lax
from jax.sharding import Mesh, PartitionSpec as P

BLK = 128
AXES = ("y", "zh", "zl", "x", "c")
RING_UP = [(i, (i + 1) % 4) for i in range(4)]
RING_DOWN = [(i, (i + 3) % 4) for i in range(4)]
SWAP = [(0, 1), (1, 0)]


def flip(bits, size):
    return [(i, i ^ bits) for i in range(size)]


def matmul(left, right):
    return jnp.dot(left, right, precision=lax.Precision.HIGH, preferred_element_type=jnp.float32)


def spread_pairs():
    pairs = []
    for source in range(128):
        y, zh, zl, x, c = source >> 5, source >> 4 & 1, source >> 3 & 1, source >> 1 & 3, source & 1
        target = ((x + y) % 4, c, y >> 1, (y & 1) * 2 + zh, zl)
        pairs.append((source, ((((target[0] * 2 + target[1]) * 2 + target[2]) * 4 + target[3]) * 2 + target[4])))
    return pairs


def gather_rows(piece, zh, shift):
    width = piece.shape[1]
    spread = lax.ppermute(piece, AXES, spread_pairs())
    other = lax.ppermute(spread, "zh", SWAP)
    pair = jnp.where(zh == 0, jnp.concatenate([spread, other]), jnp.concatenate([other, spread]))
    up = lax.ppermute(pair, "y", RING_UP)
    down = lax.ppermute(pair, "y", RING_DOWN)
    half = piece.shape[0]
    far_low = lax.ppermute(up[:half], "y", RING_UP)
    far_high = lax.ppermute(down[half:], "y", RING_DOWN)
    rows = jnp.stack([pair, down, jnp.concatenate([far_low, far_high]), up])
    return jnp.roll(rows, shift, axis=0).reshape(8 * half, width)


def scatter_sum(partial, zl, x, c):
    rows = partial.shape[0] // 16
    width = partial.shape[1]
    parts = partial.reshape(2, 4, 2, rows, width)
    take = lambda array, index, axis: lax.dynamic_index_in_dim(array, index, axis, keepdims=False)
    own = take(parts, c, 2) + lax.ppermute(take(parts, 1 - c, 2), "c", SWAP)
    at = [take(own, (x + step) % 4, 1) for step in range(4)]
    half = rows // 2
    low = lax.ppermute(at[2][:, :half], "x", RING_UP)
    high = lax.ppermute(at[2][:, half:], "x", RING_DOWN)
    up = jnp.concatenate([at[1][:, :half] + low, at[1][:, half:]], axis=1)
    down = jnp.concatenate([at[3][:, :half], at[3][:, half:] + high], axis=1)
    total = at[0] + lax.ppermute(up, "x", RING_UP) + lax.ppermute(down, "x", RING_DOWN)
    return take(total, zl, 0) + lax.ppermute(take(total, 1 - zl, 0), "zl", SWAP)


def sum_all(local, x, c):
    rows, width = local.shape
    take = lambda array, index: lax.dynamic_index_in_dim(array, index, 0, keepdims=False)
    cores = local.reshape(2, rows // 2, width)
    own = take(cores, c) + lax.ppermute(take(cores, 1 - c), "c", SWAP)
    quarters = own.reshape(4, rows // 8, width)
    got = [lax.ppermute(take(quarters, x ^ bits), "x", flip(bits, 4)) for bits in (1, 2, 3)]
    own = (take(quarters, x) + got[0]) + (got[1] + got[2])
    got = [lax.ppermute(own, "y", flip(bits, 4)) for bits in (1, 2, 3)]
    own = (own + got[0]) + (got[1] + got[2])
    got = [lax.ppermute(own, ("zh", "zl"), flip(bits, 4)) for bits in (1, 2, 3)]
    own = (own + got[0]) + (got[1] + got[2])
    got = [own] + [lax.ppermute(own, "x", flip(bits, 4)) for bits in (1, 2, 3)]
    stacked = jnp.stack(got)
    order = [take(stacked, x ^ bits) for bits in range(4)]
    own = jnp.concatenate(order)
    other = lax.ppermute(own, "c", SWAP)
    return jnp.where(c == 0, jnp.concatenate([own, other]), jnp.concatenate([other, own]))


def local_mask(blocks, device, rows):
    step = 64
    flags = jnp.repeat(blocks, BLK // step, total_repeat_length=blocks.shape[0] * (BLK // step))
    own = lax.dynamic_slice_in_dim(flags, device * (rows // step), rows // step)
    return jnp.repeat(own, step, total_repeat_length=rows).astype(jnp.float32)[:, None]


def device_step(inverse, parent_panel, child_panel, child_top, diag_parent, diag_child, parent_blocks, child_blocks):
    y, zh, zl, x, c = [lax.axis_index(name) for name in AXES]
    device = (((y * 2 + zh) * 2 + zl) * 4 + x) * 2 + c
    rows = parent_panel.shape[0]
    parent_mask = local_mask(parent_blocks, device, rows)
    child_mask = local_mask(child_blocks, device, rows)
    parent_masked = parent_panel * parent_mask
    child_masked = child_panel * child_mask
    shift = (y - (zl * 2 + x // 2)) % 4
    parent_rows = gather_rows(parent_masked, zh, shift)
    child_rows = gather_rows(child_masked, zh, shift)
    parent_image = scatter_sum(matmul(inverse, parent_rows), zl, x, c)
    child_image = scatter_sum(matmul(inverse, child_rows), zl, x, c)
    parent_column = -(parent_mask * parent_image)
    child_column = -(child_mask * (matmul(parent_column, child_top) + child_image))
    products = sum_all(
        jnp.concatenate(
            [
                matmul(parent_masked.T, parent_column),
                matmul(parent_column.T, child_masked),
                matmul(child_masked.T, child_column),
            ]
        ),
        x,
        c,
    )
    width = parent_panel.shape[1]
    parent_diagonal = diag_parent - products[:width]
    child_upper = -(matmul(parent_diagonal, child_top) + products[width : 2 * width])
    child_diagonal = diag_child - matmul(child_top.T, child_upper) - products[2 * width :]
    return parent_column, parent_diagonal, child_column, child_upper, child_diagonal


def solution(mesh):
    fine = Mesh(mesh.devices.reshape(4, 2, 2, 4, 2), AXES)
    everywhere = P(AXES, None)
    whole = P(None, None)
    return jax.shard_map(
        device_step,
        mesh=fine,
        in_specs=(P(("y", "zh"), ("zl", "x", "c")), everywhere, everywhere, whole, whole, whole, P(None), P(None)),
        out_specs=(everywhere, whole, everywhere, whole, whole),
        check_vma=False,
    )
```

time: 558 us -> 214 us (0.38)
  waiting for transfers between devices: 356 us -> 50.4 us
  blocking collectives: 29.3 us -> 0 us
  starting transfers between devices: 55.9 us -> 77.4 us
  between operations: 20.5 us -> 1.45 us
  local copies, waits for them, and re-layouts: 29.3 us -> 21.9 us
    dot_general x1 -> x0, waiting for transfers between devices: 150 us -> none  [matmul(): jnp.dot(left, right, precision=lax.Precision.HIGHEST, preferred_element_t...]
    unnamed x16 -> x0, waiting for transfers between devices: 120 us -> none
    mul x4 -> x0, waiting for transfers between devices: 85.8 us -> none  [the longest x2 46 us: reference(): parent_masked = parent_panel * parent_mask]
    ppermute x0 -> x38, starting transfers between devices: none -> 77.4 us  [the longest x2 17.5 us: gather_rows(): down = lax.ppermute(pair, 'y', RING_DOWN)]
    ppermute x0 -> x38, waiting for transfers between devices: none -> 50.4 us  [the longest x2 8.5 us: scatter_sum(): lax.ppermute(down, 'x', RING_DOWN)]
    mul x4 -> x0, starting transfers between devices: 34.5 us -> none  [the longest x2 28.5 us: reference(): parent_masked = parent_panel * parent_mask]
    unnamed x2 -> x0, blocking collectives: 29.3 us -> none
    unnamed x42 -> x52, local copies, waits for them, and re-layouts: 24.1 us -> 2.07 us
  transfers between devices with their start and end apart: 16 -> 38, of which waited for: 11 -> 24; matrix products, arithmetic and copies ran while one was open for 11% -> 30% of each run, Pallas kernels for 0% -> 0%
where the time goes in v1:
time: 214 us
  starting transfers between devices  77.4 us (36%)
  waiting for transfers between devices  50.4 us (24%)
  matrix products  44.4 us (21%)
  local copies, waits for them, and re-layouts  21.9 us (10%)
  other arithmetic  18.2 us (9%)
    dot_general x8, matrix products, matmul(): jnp.dot(left, right, precision=lax.Precision.HIGH, preferred_element_type...  44.4 us
    ppermute x2, starting transfers between devices, gather_rows(): down = lax.ppermute(pair, 'y', RING_DOWN)  17.5 us
    ppermute x2, starting transfers between devices, gather_rows(): spread = lax.ppermute(piece, AXES, spread_pairs())  9.37 us
    ppermute x2, waiting for transfers between devices, scatter_sum(): lax.ppermute(down, 'x', RING_DOWN)  8.5 us
    ppermute x2, waiting for transfers between devices, gather_rows(): down = lax.ppermute(pair, 'y', RING_DOWN)  7.7 us
    ppermute x2, starting transfers between devices, gather_rows(): other = lax.ppermute(spread, 'zh', SWAP)  6.67 us
    gather x2, local copies, waits for them, and re-layouts, local_mask(): jnp.repeat(blocks, BLK // step, total_repeat_length=blocks.shape[0] * (BL...  6.42 us
    ppermute x2, starting transfers between devices, gather_rows(): far_high = lax.ppermute(down[half:], 'y', RING_DOWN)  6.12 us
  transfers between devices with their start and end apart: 38, of which 24 were waited for; matrix products, arithmetic and copies ran while one was open for 30% of the time, Pallas kernels for 0%

profile of v1, /device:TPU:1, one launch (start us, length us, event | category | flops | bytes accessed | tf_op | source)
XLA Modules:
  0.0 213.7 jit_solution(11933549390026151919)
XLA Ops:
  1.5 1.9 scatter_custom_fusion
  4.0 3.6 %gather_fusion.1 = s32[384]{0:T(512)S(1)} fusion(s32[192]{0:T(256)} %param.29, s32[1024]{0:T(1024)S(1)} %pad_clamp_fusion), kind=kCustom, calls=%fused_computation.1.clone | custom fusion | bytes 4608 | tf_op jit(solution)/shard_map/jit(_take)/gather | solution.py:82
  8.4 2.8 %gather_fusion = s32[384]{0:T(512)S(1)} fusion(s32[192]{0:T(256)S(1)} %copy-done.1, s32[1024]{0:T(1024)S(1)} %pad_clamp_fusion), kind=kCustom, calls=%fused_computation.clone | custom fusion | bytes 4608 | tf_op jit(solution)/shard_map/jit(_take)/gather | solution.py:82
  12.0 3.9 %select_convert_fusion = (f32[192]{0:T(256)S(1)}, f32[192]{0:T(256)S(1)}) fusion(s32[]{:T(128)} %bitcast.25, s32[]{:T(128)} %bitcast.24, s32[]{:T(128)} %bitcast.23, s32[256]{0:T(256)S(1)} %add_bitcast_fusion, s32[]{:T(128)} %bitcast.6, s32[]{:T(128)} %bitcast.5, s32[]{:T(128)} %bitcast.4), kind=kLoop, calls=%fused_computation.114 | loop fusion | flops 3264 | bytes 2328 | tf_op jit(solution)/shard_map/convert_element_type | solution.py:84
  16.0 6.9 %collective-permute-start = (f32[192,256]{1,0:T(8,128)S(1)}, f32[192,256]{1,0:T(8,128)S(1)}, u32[]{:S(2)}, u32[]{:S(2)}) collective-permute-start(f32[192,256]{1,0:T(8,128)S(1)} %broadcast_multiply_fusion.1), channel_id=1, source_target_pairs={{0,0},{1,16},{2,32},{3,48},{4,64},{5,80},{6,96},{7,112},{8,1},{9,1... | collective-permute-start | bytes 589832 | tf_op jit(solution)/shard_map/ppermute | solution.py:32
  23.0 2.5 %collective-permute-start.12 = (f32[192,256]{1,0:T(8,128)S(1)}, f32[192,256]{1,0:T(8,128)S(1)}, u32[]{:S(2)}, u32[]{:S(2)}) collective-permute-start(f32[192,256]{1,0:T(8,128)S(1)} %broadcast_multiply_fusion), channel_id=1, source_target_pairs={{0,0},{1,16},{2,32},{3,48},{4,64},{5,80},{6,96},{7,112},{8,1},{9,1... | collective-permute-start | bytes 589832 | tf_op jit(solution)/shard_map/ppermute | solution.py:32
  25.5 3.3 %collective-permute-start.1 = (f32[192,256]{1,0:T(8,128)S(1)}, f32[192,256]{1,0:T(8,128)S(1)}, u32[]{:S(2)}, u32[]{:S(2)}) collective-permute-start(f32[192,256]{1,0:T(8,128)S(1)} %collective-permute-done), channel_id=1, source_target_pairs={{0,16},{16,0},{1,17},{17,1},{2,18},{18,2},{3,19},{19,3},{4,20},{20... | collective-permute-start | bytes 589832 | tf_op jit(solution)/shard_map/ppermute | solution.py:33
  28.8 1.2 collective-permute-done.12
  30.0 3.4 %collective-permute-start.13 = (f32[192,256]{1,0:T(8,128)S(1)}, f32[192,256]{1,0:T(8,128)S(1)}, u32[]{:S(2)}, u32[]{:S(2)}) collective-permute-start(f32[192,256]{1,0:T(8,128)S(1)} %collective-permute-done.12), channel_id=1, source_target_pairs={{0,16},{16,0},{1,17},{17,1},{2,18},{18,2},{3,19},{19,3},{4,20},{20... | collective-permute-start | bytes 589832 | tf_op jit(solution)/shard_map/ppermute | solution.py:33
  33.4 1.0 collective-permute-done.1
  35.2 13.8 %collective-permute-start.2 = (f32[384,256]{1,0:T(8,128)}, f32[384,256]{1,0:T(8,128)S(1)}, u32[]{:S(2)}, u32[]{:S(2)}) collective-permute-start(f32[384,256]{1,0:T(8,128)} %maximum_select_fusion.1), channel_id=1, source_target_pairs={{0,96},{32,0},{64,32},{96,64},{1,97},{33,1},{65,33},{97,65},{2,98}... | collective-permute-start | bytes 1179656 | tf_op jit(solution)/shard_map/ppermute | solution.py:36
  49.0 3.8 %collective-permute-start.14 = (f32[384,256]{1,0:T(8,128)S(1)}, f32[384,256]{1,0:T(8,128)S(1)}, u32[]{:S(2)}, u32[]{:S(2)}) collective-permute-start(f32[384,256]{1,0:T(8,128)S(1)} %maximum_select_fusion.3), channel_id=1, source_target_pairs={{0,96},{32,0},{64,32},{96,64},{1,97},{33,1},{65,33},{97,65},{2,98}... | collective-permute-start | bytes 1179656 | tf_op jit(solution)/shard_map/ppermute | solution.py:36
  52.8 3.3 %collective-permute-done.2 = f32[384,256]{1,0:T(8,128)S(1)} collective-permute-done((f32[384,256]{1,0:T(8,128)}, f32[384,256]{1,0:T(8,128)S(1)}, u32[]{:S(2)}, u32[]{:S(2)}) %collective-permute-start.2) | collective-permute-done | bytes 393248 | tf_op jit(solution)/shard_map/ppermute | solution.py:36
  56.1 3.1 %collective-permute-start.5 = (f32[192,256]{1,0:T(8,128)S(1)}, f32[192,256]{1,0:T(8,128)S(1)}, u32[]{:S(2)}, u32[]{:S(2)}) collective-permute-start(f32[192,256]{1,0:T(8,128)S(1)} %slice.160), channel_id=1, source_target_pairs={{0,96},{32,0},{64,32},{96,64},{1,97},{33,1},{65,33},{97,65},{2,98}... | collective-permute-start | bytes 589832 | tf_op jit(solution)/shard_map/ppermute | solution.py:39
  60.2 4.4 %collective-permute-done.14 = f32[384,256]{1,0:T(8,128)S(1)} collective-permute-done((f32[384,256]{1,0:T(8,128)S(1)}, f32[384,256]{1,0:T(8,128)S(1)}, u32[]{:S(2)}, u32[]{:S(2)}) %collective-permute-start.14) | collective-permute-done | bytes 393248 | tf_op jit(solution)/shard_map/ppermute | solution.py:36
  65.3 3.0 %collective-permute-start.17 = (f32[192,256]{1,0:T(8,128)}, f32[192,256]{1,0:T(8,128)}, u32[]{:S(2)}, u32[]{:S(2)}) collective-permute-start(f32[192,256]{1,0:T(8,128)} %slice.168), channel_id=1, source_target_pairs={{0,96},{32,0},{64,32},{96,64},{1,97},{33,1},{65,33},{97,65},{2,98}... | collective-permute-start | bytes 589832 | tf_op jit(solution)/shard_map/ppermute | solution.py:39
  69.0 2.5 %collective-permute-done.4 = f32[192,256]{1,0:T(8,128)S(1)} collective-permute-done((f32[192,256]{1,0:T(8,128)S(1)}, f32[192,256]{1,0:T(8,128)S(1)}, u32[]{:S(2)}, u32[]{:S(2)}) %collective-permute-start.4) | collective-permute-done | bytes 196640 | tf_op jit(solution)/shard_map/ppermute | solution.py:38
  71.5 0.9 fusion.10
  72.5 20.7 %convolution_bitcast_fusion.1 = f32[3072,256]{0,1:T(8,128)} fusion(f32[1536,256]{1,0:T(8,128)S(1)} %bitcast.132, f32[3072,1536]{1,0:T(8,128)} %param.22), kind=kOutput, calls=%fused_computation.4 | convolution fusion | flops 7247757312 | bytes 23592960 | tf_op jit(solution)/shard_map/dot_general | solution.py:18
  93.1 2.4 %copy.18 = f32[3072,256]{1,0:T(8,128)S(1)} copy(f32[3072,256]{0,1:T(8,128)} %convolution_bitcast_fusion.1) | data formatting | bytes 6291456 | tf_op jit(solution)/shard_map/dot_general | solution.py:18
  95.5 1.4 dynamic-slice_bitcast_fusion.1
  96.9 4.1 %collective-permute-start.6 = (f32[2,4,192,256]{3,2,1,0:T(8,128)}, f32[2,4,192,256]{3,2,1,0:T(8,128)}, u32[]{:S(2)}, u32[]{:S(2)}) collective-permute-start(f32[2,4,192,256]{3,2,1,0:T(8,128)} %dynamic-slice_bitcast_fusion.1), channel_id=1, source_target_pairs={{0,1},{1,0},{2,3},{3,2},{4,5},{5,4},{6,7},{7,6},{8,9},{9,8},{10,11... | collective-permute-start | bytes 4718600 | tf_op jit(solution)/shard_map/ppermute | solution.py:49
  101.0 1.0 maximum_bitcast_fusion.1
  102.0 0.9 fusion.3
  102.9 20.7 %convolution_bitcast_fusion = f32[3072,256]{0,1:T(8,128)} fusion(f32[1536,256]{1,0:T(8,128)S(1)} %bitcast.131, f32[3072,1536]{1,0:T(8,128)} %param.22), kind=kOutput, calls=%fused_computation.3 | convolution fusion | flops 7247757312 | bytes 23592960 | tf_op jit(solution)/shard_map/dot_general | solution.py:18
  123.7 3.6 %copy.19 = f32[3072,256]{1,0:T(8,128)} copy(f32[3072,256]{0,1:T(8,128)} %convolution_bitcast_fusion) | data formatting | bytes 6291456 | tf_op jit(solution)/shard_map/dot_general | solution.py:18
  127.2 2.7 %dynamic-slice_bitcast_fusion = f32[2,4,192,256]{3,2,1,0:T(8,128)} fusion(f32[2,4,2,192,256]{4,3,2,1,0:T(8,128)} %bitcast.129, s32[]{:T(128)S(6)} %select_n.173), kind=kLoop, calls=%fused_computation.37 | loop fusion | bytes 3145732 | tf_op jit(solution)/shard_map/jit(dynamic_index_in_dim)/squeeze | solution.py:48
  129.9 1.6 bitcast_add_fusion.1
  131.7 1.0 copy-done.3
  132.7 1.4 collective-permute-start.9
  134.2 1.6 bitcast_add_fusion
  135.9 2.7 %collective-permute-start.21 = (f32[2,96,256]{2,1,0:T(8,128)S(1)}, f32[2,96,256]{2,1,0:T(8,128)S(1)}, u32[]{:S(2)}, u32[]{:S(2)}) collective-permute-start(f32[2,96,256]{2,1,0:T(8,128)S(1)} %get-tuple-element.72), channel_id=1, source_target_pairs={{0,6},{2,0},{4,2},{6,4},{1,7},{3,1},{5,3},{7,5},{8,14},{10,8},{12,... | collective-permute-start | bytes 589832 | tf_op jit(solution)/shard_map/ppermute | solution.py:53
  138.7 2.7 %collective-permute-start.10 = (f32[2,192,256]{2,1,0:T(8,128)S(1)}, f32[2,192,256]{2,1,0:T(8,128)}, u32[]{:S(2)}, u32[]{:S(2)}) collective-permute-start(f32[2,192,256]{2,1,0:T(8,128)S(1)} %pad_maximum_fusion.2), channel_id=1, source_target_pairs={{0,6},{2,0},{4,2},{6,4},{1,7},{3,1},{5,3},{7,5},{8,14},{10,8},{12,... | collective-permute-start | bytes 1179656 | tf_op jit(solution)/shard_map/ppermute | solution.py:56
  141.6 1.3 collective-permute-done.21
  143.0 2.4 %collective-permute-start.22 = (f32[2,192,256]{2,1,0:T(8,128)S(1)}, f32[2,192,256]{2,1,0:T(8,128)}, u32[]{:S(2)}, u32[]{:S(2)}) collective-permute-start(f32[2,192,256]{2,1,0:T(8,128)S(1)} %pad_maximum_fusion.4), channel_id=1, source_target_pairs={{0,6},{2,0},{4,2},{6,4},{1,7},{3,1},{5,3},{7,5},{8,14},{10,8},{12,... | collective-permute-start | bytes 1179656 | tf_op jit(solution)/shard_map/ppermute | solution.py:56
  145.6 5.9 %collective-permute-done.10 = f32[2,192,256]{2,1,0:T(8,128)} collective-permute-done((f32[2,192,256]{2,1,0:T(8,128)S(1)}, f32[2,192,256]{2,1,0:T(8,128)}, u32[]{:S(2)}, u32[]{:S(2)}) %collective-permute-start.10) | collective-permute-done | bytes 393248 | tf_op jit(solution)/shard_map/ppermute | solution.py:56
  151.5 2.6 %collective-permute-done.8 = f32[2,192,256]{2,1,0:T(8,128)} collective-permute-done((f32[2,192,256]{2,1,0:T(8,128)S(1)}, f32[2,192,256]{2,1,0:T(8,128)}, u32[]{:S(2)}, u32[]{:S(2)}) %collective-permute-start.8) | collective-permute-done | bytes 393248 | tf_op jit(solution)/shard_map/ppermute | solution.py:56
  154.0 1.3 fusion.19
  155.4 1.9 collective-permute-start.11
  157.3 2.6 %collective-permute-done.22 = f32[2,192,256]{2,1,0:T(8,128)} collective-permute-done((f32[2,192,256]{2,1,0:T(8,128)S(1)}, f32[2,192,256]{2,1,0:T(8,128)}, u32[]{:S(2)}, u32[]{:S(2)}) %collective-permute-start.22) | collective-permute-done | bytes 393248 | tf_op jit(solution)/shard_map/ppermute | solution.py:56
  159.9 2.6 %collective-permute-done.20 = f32[2,192,256]{2,1,0:T(8,128)} collective-permute-done((f32[2,192,256]{2,1,0:T(8,128)S(1)}, f32[2,192,256]{2,1,0:T(8,128)}, u32[]{:S(2)}, u32[]{:S(2)}) %collective-permute-start.20) | collective-permute-done | bytes 393248 | tf_op jit(solution)/shard_map/ppermute | solution.py:56
  162.5 1.2 fusion.18
  163.7 2.1 collective-permute-start.23
  166.8 2.6 %collective-permute-done.23 = f32[192,256]{1,0:T(8,128)S(1)} collective-permute-done((f32[192,256]{1,0:T(8,128)S(1)}, f32[192,256]{1,0:T(8,128)S(1)}, u32[]{:S(2)}, u32[]{:S(2)}) %collective-permute-start.23) | collective-permute-done | bytes 196640 | tf_op jit(solution)/shard_map/ppermute | solution.py:57
  170.3 2.3 %collective-permute-start.24 = (f32[384,256]{1,0:T(8,128)S(1)}, f32[384,256]{1,0:T(8,128)S(1)}, u32[]{:S(2)}, u32[]{:S(2)}) collective-permute-start(f32[384,256]{1,0:T(8,128)S(1)} %dynamic-slice_bitcast_fusion.2), channel_id=1, source_target_pairs={{0,1},{1,0},{2,3},{3,2},{4,5},{5,4},{6,7},{7,6},{8,9},{9,8},{10,11... | collective-permute-start | bytes 1179656 | tf_op jit(solution)/shard_map/ppermute | solution.py:64
  172.6 1.3 collective-permute-done.24
  174.1 1.0 collective-permute-start.26
  175.2 2.8 %collective-permute-start.27 = (f32[96,256]{1,0:T(8,128)S(1)}, f32[96,256]{1,0:T(8,128)S(1)}, u32[]{:S(2)}, u32[]{:S(2)}) collective-permute-start(f32[96,256]{1,0:T(8,128)S(1)} %get-tuple-element.66), channel_id=1, source_target_pairs={{0,6},{2,4},{4,2},{6,0},{1,7},{3,5},{5,3},{7,1},{8,14},{10,12},{12... | collective-permute-start | bytes 294920 | tf_op jit(solution)/shard_map/ppermute | solution.py:66
  178.1 1.8 collective-permute-done.26
  179.9 2.8 %collective-permute-done.27 = f32[96,256]{1,0:T(8,128)S(1)} collective-permute-done((f32[96,256]{1,0:T(8,128)S(1)}, f32[96,256]{1,0:T(8,128)S(1)}, u32[]{:S(2)}, u32[]{:S(2)}) %collective-permute-start.27) | collective-permute-done | bytes 98336 | tf_op jit(solution)/shard_map/ppermute | solution.py:66
  182.8 1.9 collective-permute-start.30
  185.4 2.8 %collective-permute-done.29 = f32[96,256]{1,0:T(8,128)S(1)} collective-permute-done((f32[96,256]{1,0:T(8,128)S(1)}, f32[96,256]{1,0:T(8,128)S(1)}, u32[]{:S(2)}, u32[]{:S(2)}) %collective-permute-start.29) | collective-permute-done | bytes 98336 | tf_op jit(solution)/shard_map/ppermute | solution.py:68
  188.1 2.5 %collective-permute-done.30 = f32[96,256]{1,0:T(8,128)S(1)} collective-permute-done((f32[96,256]{1,0:T(8,128)S(1)}, f32[96,256]{1,0:T(8,128)S(1)}, u32[]{:S(2)}, u32[]{:S(2)}) %collective-permute-start.30) | collective-permute-done | bytes 98336 | tf_op jit(solution)/shard_map/ppermute | solution.py:68
  190.7 2.8 %collective-permute-start.32 = (f32[96,256]{1,0:T(8,128)S(1)}, f32[96,256]{1,0:T(8,128)S(1)}, u32[]{:S(2)}, u32[]{:S(2)}) collective-permute-start(f32[96,256]{1,0:T(8,128)S(1)} %add_add_fusion.1), channel_id=1, source_target_pairs={{0,16},{8,24},{16,0},{24,8},{1,17},{9,25},{17,1},{25,9},{2,18},{10... | collective-permute-start | bytes 294920 | tf_op jit(solution)/shard_map/ppermute | solution.py:70
  193.5 1.3 collective-permute-start.33
  194.8 1.0 collective-permute-done.32
  195.8 2.4 %collective-permute-done.33 = f32[96,256]{1,0:T(8,128)S(1)} collective-permute-done((f32[96,256]{1,0:T(8,128)S(1)}, f32[96,256]{1,0:T(8,128)S(1)}, u32[]{:S(2)}, u32[]{:S(2)}) %collective-permute-start.33) | collective-permute-done | bytes 98336 | tf_op jit(solution)/shard_map/ppermute | solution.py:70
  198.3 2.5 %collective-permute-start.36 = (f32[96,256]{1,0:T(8,128)S(1)}, f32[96,256]{1,0:T(8,128)S(1)}, u32[]{:S(2)}, u32[]{:S(2)}) collective-permute-start(f32[96,256]{1,0:T(8,128)S(1)} %add_add_fusion), channel_id=1, source_target_pairs={{0,6},{2,4},{4,2},{6,0},{1,7},{3,5},{5,3},{7,1},{8,14},{10,12},{12... | collective-permute-start | bytes 294920 | tf_op jit(solution)/shard_map/ppermute | solution.py:72
  200.8 0.8 collective-permute-start.34
  201.6 1.8 collective-permute-done.36
  203.4 2.5 %collective-permute-done.35 = f32[96,256]{1,0:T(8,128)S(1)} collective-permute-done((f32[96,256]{1,0:T(8,128)S(1)}, f32[96,256]{1,0:T(8,128)S(1)}, u32[]{:S(2)}, u32[]{:S(2)}) %collective-permute-start.35) | collective-permute-done | bytes 98336 | tf_op jit(solution)/shard_map/ppermute | solution.py:72
  206.0 3.8 %collective-permute-start.37 = (f32[384,256]{1,0:T(8,128)S(1)}, f32[384,256]{1,0:T(8,128)S(1)}, u32[]{:S(2)}, u32[]{:S(2)}) collective-permute-start(f32[384,256]{1,0:T(8,128)S(1)} %pad_maximum_fusion.6), channel_id=1, source_target_pairs={{0,1},{1,0},{2,3},{3,2},{4,5},{5,4},{6,7},{7,6},{8,9},{9,8},{10,11... | collective-permute-start | bytes 1179656 | tf_op jit(solution)/shard_map/ppermute | solution.py:76
  209.8 1.3 collective-permute-done.37
  212.6 1.1 slice_subtract_fusion
  (143 shorter events, 11.8 us)
Async XLA Ops:
  0.6 168.8 %copy-start = (f32[256,256]{1,0:T(8,128)S(1)}, f32[256,256]{1,0:T(8,128)}, u32[]{:S(2)}) copy-start(f32[256,256]{1,0:T(8,128)} %param.25) | copy-start | bytes 786436
  0.6 7.7 %copy-start.1 = (s32[192]{0:T(256)S(1)}, s32[192]{0:T(256)}, u32[]{:S(2)}) copy-start(s32[192]{0:T(256)} %param.28) | copy-start | bytes 2308
  7.6 4.3 %copy-start.21 = (s32[2,128]{1,0:T(2,128)S(1)}, s32[2,128]{1,0:T(2,128)}, u32[]{:S(2)}) copy-start(s32[2,128]{1,0:T(2,128)} %constant.310.clone.1) | copy-start | bytes 3076
  7.6 8.2 %copy-start.19 = (f32[192,256]{1,0:T(8,128)S(1)}, f32[192,256]{1,0:T(8,128)}, u32[]{:S(2)}) copy-start(f32[192,256]{1,0:T(8,128)} %param.23) | copy-start | bytes 589828
  7.6 15.2 %copy-start.20 = (f32[192,256]{1,0:T(8,128)S(1)}, f32[192,256]{1,0:T(8,128)}, u32[]{:S(2)}) copy-start(f32[192,256]{1,0:T(8,128)} %param.24) | copy-start | bytes 589828
  16.0 6.9 %copy-start.15 = (f32[192,256]{1,0:T(8,128)}, f32[192,256]{1,0:T(8,128)S(1)}, u32[]{:S(2)}) copy-start(f32[192,256]{1,0:T(8,128)S(1)} %broadcast_multiply_fusion.1) | copy-start | bytes 589828
  16.0 9.5 %collective-permute-start = (f32[192,256]{1,0:T(8,128)S(1)}, f32[192,256]{1,0:T(8,128)S(1)}, u32[]{:S(2)}, u32[]{:S(2)}) collective-permute-start(f32[192,256]{1,0:T(8,128)S(1)} %broadcast_multiply_fusion.1), channel_id=1, source_target_pairs={{0,0},{1,16},{2,32},{3,48},{4,64},{5,80},{6,96},{7,112},{8,1},{9,1... | collective-permute-start | bytes 589832 | tf_op jit(solution)/shard_map/ppermute | solution.py:32
  23.0 36.4 %copy-start.5 = (f32[192,256]{1,0:T(8,128)}, f32[192,256]{1,0:T(8,128)S(1)}, u32[]{:S(2)}) copy-start(f32[192,256]{1,0:T(8,128)S(1)} %broadcast_multiply_fusion) | copy-start | bytes 589828
  23.0 7.0 %collective-permute-start.12 = (f32[192,256]{1,0:T(8,128)S(1)}, f32[192,256]{1,0:T(8,128)S(1)}, u32[]{:S(2)}, u32[]{:S(2)}) collective-permute-start(f32[192,256]{1,0:T(8,128)S(1)} %broadcast_multiply_fusion), channel_id=1, source_target_pairs={{0,0},{1,16},{2,32},{3,48},{4,64},{5,80},{6,96},{7,112},{8,1},{9,1... | collective-permute-start | bytes 589832 | tf_op jit(solution)/shard_map/ppermute | solution.py:32
  25.5 8.9 %collective-permute-start.1 = (f32[192,256]{1,0:T(8,128)S(1)}, f32[192,256]{1,0:T(8,128)S(1)}, u32[]{:S(2)}, u32[]{:S(2)}) collective-permute-start(f32[192,256]{1,0:T(8,128)S(1)} %collective-permute-done), channel_id=1, source_target_pairs={{0,16},{16,0},{1,17},{17,1},{2,18},{18,2},{3,19},{19,3},{4,20},{20... | collective-permute-start | bytes 589832 | tf_op jit(solution)/shard_map/ppermute | solution.py:33
  30.0 19.0 %collective-permute-start.13 = (f32[192,256]{1,0:T(8,128)S(1)}, f32[192,256]{1,0:T(8,128)S(1)}, u32[]{:S(2)}, u32[]{:S(2)}) collective-permute-start(f32[192,256]{1,0:T(8,128)S(1)} %collective-permute-done.12), channel_id=1, source_target_pairs={{0,16},{16,0},{1,17},{17,1},{2,18},{18,2},{3,19},{19,3},{4,20},{20... | collective-permute-start | bytes 589832 | tf_op jit(solution)/shard_map/ppermute | solution.py:33
  35.2 20.9 %collective-permute-start.2 = (f32[384,256]{1,0:T(8,128)}, f32[384,256]{1,0:T(8,128)S(1)}, u32[]{:S(2)}, u32[]{:S(2)}) collective-permute-start(f32[384,256]{1,0:T(8,128)} %maximum_select_fusion.1), channel_id=1, source_target_pairs={{0,96},{32,0},{64,32},{96,64},{1,97},{33,1},{65,33},{97,65},{2,98}... | collective-permute-start | bytes 1179656 | tf_op jit(solution)/shard_map/ppermute | solution.py:36
  49.0 10.3 %collective-permute-start.3 = (f32[384,256]{1,0:T(8,128)}, f32[384,256]{1,0:T(8,128)S(1)}, u32[]{:S(2)}, u32[]{:S(2)}) collective-permute-start(f32[384,256]{1,0:T(8,128)} %maximum_select_fusion.1), channel_id=1, source_target_pairs={{0,32},{32,64},{64,96},{96,0},{1,33},{33,65},{65,97},{97,1},{2,34}... | collective-permute-start | bytes 1179656 | tf_op jit(solution)/shard_map/ppermute | solution.py:35
  49.0 15.5 %collective-permute-start.14 = (f32[384,256]{1,0:T(8,128)S(1)}, f32[384,256]{1,0:T(8,128)S(1)}, u32[]{:S(2)}, u32[]{:S(2)}) collective-permute-start(f32[384,256]{1,0:T(8,128)S(1)} %maximum_select_fusion.3), channel_id=1, source_target_pairs={{0,96},{32,0},{64,32},{96,64},{1,97},{33,1},{65,33},{97,65},{2,98}... | collective-permute-start | bytes 1179656 | tf_op jit(solution)/shard_map/ppermute | solution.py:36
  52.8 15.5 %collective-permute-start.15 = (f32[384,256]{1,0:T(8,128)S(1)}, f32[384,256]{1,0:T(8,128)S(1)}, u32[]{:S(2)}, u32[]{:S(2)}) collective-permute-start(f32[384,256]{1,0:T(8,128)S(1)} %maximum_select_fusion.3), channel_id=1, source_target_pairs={{0,32},{32,64},{64,96},{96,0},{1,33},{33,65},{65,97},{97,1},{2,34}... | collective-permute-start | bytes 1179656 | tf_op jit(solution)/shard_map/ppermute | solution.py:35
  56.1 12.9 %collective-permute-start.5 = (f32[192,256]{1,0:T(8,128)S(1)}, f32[192,256]{1,0:T(8,128)S(1)}, u32[]{:S(2)}, u32[]{:S(2)}) collective-permute-start(f32[192,256]{1,0:T(8,128)S(1)} %slice.160), channel_id=1, source_target_pairs={{0,96},{32,0},{64,32},{96,64},{1,97},{33,1},{65,33},{97,65},{2,98}... | collective-permute-start | bytes 589832 | tf_op jit(solution)/shard_map/ppermute | solution.py:39
  59.3 12.3 %collective-permute-start.4 = (f32[192,256]{1,0:T(8,128)S(1)}, f32[192,256]{1,0:T(8,128)S(1)}, u32[]{:S(2)}, u32[]{:S(2)}) collective-permute-start(f32[192,256]{1,0:T(8,128)S(1)} %slice.159), channel_id=1, source_target_pairs={{0,32},{32,64},{64,96},{96,0},{1,33},{33,65},{65,97},{97,1},{2,34}... | collective-permute-start | bytes 589832 | tf_op jit(solution)/shard_map/ppermute | solution.py:38
  64.6 7.9 %copy-start.10 = (f32[384,256]{1,0:T(8,128)}, f32[384,256]{1,0:T(8,128)S(1)}, u32[]{:S(2)}) copy-start(f32[384,256]{1,0:T(8,128)S(1)} %collective-permute-done.14) | copy-start | bytes 1179652
  65.3 35.7 %collective-permute-start.17 = (f32[192,256]{1,0:T(8,128)}, f32[192,256]{1,0:T(8,128)}, u32[]{:S(2)}, u32[]{:S(2)}) collective-permute-start(f32[192,256]{1,0:T(8,128)} %slice.168), channel_id=1, source_target_pairs={{0,96},{32,0},{64,32},{96,64},{1,97},{33,1},{65,33},{97,65},{2,98}... | collective-permute-start | bytes 589832 | tf_op jit(solution)/shard_map/ppermute | solution.py:39
  68.3 4.1 %copy-start.12 = (f32[384,256]{1,0:T(8,128)}, f32[384,256]{1,0:T(8,128)S(1)}, u32[]{:S(2)}) copy-start(f32[384,256]{1,0:T(8,128)S(1)} %collective-permute-done.15) | copy-start | bytes 1179652
  69.0 31.9 %collective-permute-start.16 = (f32[192,256]{1,0:T(8,128)}, f32[192,256]{1,0:T(8,128)}, u32[]{:S(2)}, u32[]{:S(2)}) collective-permute-start(f32[192,256]{1,0:T(8,128)} %slice.167), channel_id=1, source_target_pairs={{0,32},{32,64},{64,96},{96,0},{1,33},{33,65},{65,97},{97,1},{2,34}... | collective-permute-start | bytes 589832 | tf_op jit(solution)/shard_map/ppermute | solution.py:38
  95.5 6.5 %copy-start.7 = (f32[1,384,256]{2,1,0:T(8,128)S(1)}, f32[1,384,256]{2,1,0:T(8,128)}, u32[]{:S(2)}) copy-start(f32[1,384,256]{2,1,0:T(8,128)} %maximum_select_fusion.2) | copy-start | bytes 1179652
  95.5 6.5 %copy-start.11 = (f32[384,256]{1,0:T(8,128)S(1)}, f32[384,256]{1,0:T(8,128)}, u32[]{:S(2)}) copy-start(f32[384,256]{1,0:T(8,128)} %copy-done.10) | copy-start | bytes 1179652
  95.5 6.5 %copy-start.13 = (f32[384,256]{1,0:T(8,128)S(1)}, f32[384,256]{1,0:T(8,128)}, u32[]{:S(2)}) copy-start(f32[384,256]{1,0:T(8,128)} %copy-done.12) | copy-start | bytes 1179652
  96.9 33.0 %collective-permute-start.6 = (f32[2,4,192,256]{3,2,1,0:T(8,128)}, f32[2,4,192,256]{3,2,1,0:T(8,128)}, u32[]{:S(2)}, u32[]{:S(2)}) collective-permute-start(f32[2,4,192,256]{3,2,1,0:T(8,128)} %dynamic-slice_bitcast_fusion.1), channel_id=1, source_target_pairs={{0,1},{1,0},{2,3},{3,2},{4,5},{5,4},{6,7},{7,6},{8,9},{9,8},{10,11... | collective-permute-start | bytes 4718600 | tf_op jit(solution)/shard_map/ppermute | solution.py:49
  129.9 4.3 %collective-permute-start.18 = (f32[2,4,192,256]{3,2,1,0:T(8,128)}, f32[2,4,192,256]{3,2,1,0:T(8,128)}, u32[]{:S(2)}, u32[]{:S(2)}) collective-permute-start(f32[2,4,192,256]{3,2,1,0:T(8,128)} %dynamic-slice_bitcast_fusion), channel_id=1, source_target_pairs={{0,1},{1,0},{2,3},{3,2},{4,5},{5,4},{6,7},{7,6},{8,9},{9,8},{10,11... | collective-permute-start | bytes 4718600 | tf_op jit(solution)/shard_map/ppermute | solution.py:49
  131.5 1.2 copy-start.3
  131.5 2.6 %copy-start.2 = (f32[3072,256]{1,0:T(8,128)S(1)}, f32[3072,256]{1,0:T(8,128)}, u32[]{:S(2)}) copy-start(f32[3072,256]{1,0:T(8,128)} %copy.19) | copy-start | bytes 9437188
  132.7 6.0 %collective-permute-start.9 = (f32[2,96,256]{2,1,0:T(8,128)S(1)}, f32[2,96,256]{2,1,0:T(8,128)S(1)}, u32[]{:S(2)}, u32[]{:S(2)}) collective-permute-start(f32[2,96,256]{2,1,0:T(8,128)S(1)} %get-tuple-element.78), channel_id=1, source_target_pairs={{0,6},{2,0},{4,2},{6,4},{1,7},{3,1},{5,3},{7,5},{8,14},{10,8},{12,... | collective-permute-start | bytes 589832 | tf_op jit(solution)/shard_map/ppermute | solution.py:53
  134.1 7.3 %collective-permute-start.7 = (f32[2,96,256]{2,1,0:T(8,128)S(1)}, f32[2,96,256]{2,1,0:T(8,128)S(1)}, u32[]{:S(2)}, u32[]{:S(2)}) collective-permute-start(f32[2,96,256]{2,1,0:T(8,128)S(1)} %get-tuple-element.77), channel_id=1, source_target_pairs={{0,2},{2,4},{4,6},{6,0},{1,3},{3,5},{5,7},{7,1},{8,10},{10,12},{12... | collective-permute-start | bytes 589832 | tf_op jit(solution)/shard_map/ppermute | solution.py:52
  135.9 7.0 %collective-permute-start.21 = (f32[2,96,256]{2,1,0:T(8,128)S(1)}, f32[2,96,256]{2,1,0:T(8,128)S(1)}, u32[]{:S(2)}, u32[]{:S(2)}) collective-permute-start(f32[2,96,256]{2,1,0:T(8,128)S(1)} %get-tuple-element.72), channel_id=1, source_target_pairs={{0,6},{2,0},{4,2},{6,4},{1,7},{3,1},{5,3},{7,5},{8,14},{10,8},{12,... | collective-permute-start | bytes 589832 | tf_op jit(solution)/shard_map/ppermute | solution.py:53
  138.6 6.8 %collective-permute-start.19 = (f32[2,96,256]{2,1,0:T(8,128)S(1)}, f32[2,96,256]{2,1,0:T(8,128)S(1)}, u32[]{:S(2)}, u32[]{:S(2)}) collective-permute-start(f32[2,96,256]{2,1,0:T(8,128)S(1)} %get-tuple-element.71), channel_id=1, source_target_pairs={{0,2},{2,4},{4,6},{6,0},{1,3},{3,5},{5,7},{7,1},{8,10},{10,12},{12... | collective-permute-start | bytes 589832 | tf_op jit(solution)/shard_map/ppermute | solution.py:52
  138.7 12.7 %collective-permute-start.10 = (f32[2,192,256]{2,1,0:T(8,128)S(1)}, f32[2,192,256]{2,1,0:T(8,128)}, u32[]{:S(2)}, u32[]{:S(2)}) collective-permute-start(f32[2,192,256]{2,1,0:T(8,128)S(1)} %pad_maximum_fusion.2), channel_id=1, source_target_pairs={{0,6},{2,0},{4,2},{6,4},{1,7},{3,1},{5,3},{7,5},{8,14},{10,8},{12,... | collective-permute-start | bytes 1179656 | tf_op jit(solution)/shard_map/ppermute | solution.py:56
  141.5 12.5 %collective-permute-start.8 = (f32[2,192,256]{2,1,0:T(8,128)S(1)}, f32[2,192,256]{2,1,0:T(8,128)}, u32[]{:S(2)}, u32[]{:S(2)}) collective-permute-start(f32[2,192,256]{2,1,0:T(8,128)S(1)} %pad_maximum_fusion.1), channel_id=1, source_target_pairs={{0,2},{2,4},{4,6},{6,0},{1,3},{3,5},{5,7},{7,1},{8,10},{10,12},{12... | collective-permute-start | bytes 1179656 | tf_op jit(solution)/shard_map/ppermute | solution.py:56
  143.0 16.9 %collective-permute-start.22 = (f32[2,192,256]{2,1,0:T(8,128)S(1)}, f32[2,192,256]{2,1,0:T(8,128)}, u32[]{:S(2)}, u32[]{:S(2)}) collective-permute-start(f32[2,192,256]{2,1,0:T(8,128)S(1)} %pad_maximum_fusion.4), channel_id=1, source_target_pairs={{0,6},{2,0},{4,2},{6,4},{1,7},{3,1},{5,3},{7,5},{8,14},{10,8},{12,... | collective-permute-start | bytes 1179656 | tf_op jit(solution)/shard_map/ppermute | solution.py:56
  145.5 17.0 %collective-permute-start.20 = (f32[2,192,256]{2,1,0:T(8,128)S(1)}, f32[2,192,256]{2,1,0:T(8,128)}, u32[]{:S(2)}, u32[]{:S(2)}) collective-permute-start(f32[2,192,256]{2,1,0:T(8,128)S(1)} %pad_maximum_fusion.3), channel_id=1, source_target_pairs={{0,2},{2,4},{4,6},{6,0},{1,3},{3,5},{5,7},{7,1},{8,10},{10,12},{12... | collective-permute-start | bytes 1179656 | tf_op jit(solution)/shard_map/ppermute | solution.py:56
  155.4 10.6 %copy-start.6 = (f32[192,256]{1,0:T(8,128)S(1)}, f32[192,256]{1,0:T(8,128)}, u32[]{:S(2)}) copy-start(f32[192,256]{1,0:T(8,128)} %copy-done.5) | copy-start | bytes 589828
  155.4 11.0 %copy-start.16 = (f32[192,256]{1,0:T(8,128)S(1)}, f32[192,256]{1,0:T(8,128)}, u32[]{:S(2)}) copy-start(f32[192,256]{1,0:T(8,128)} %copy-done.15) | copy-start | bytes 589828
  155.4 10.4 %collective-permute-start.11 = (f32[192,256]{1,0:T(8,128)S(1)}, f32[192,256]{1,0:T(8,128)S(1)}, u32[]{:S(2)}, u32[]{:S(2)}) collective-permute-start(f32[192,256]{1,0:T(8,128)S(1)} %dynamic-slice_bitcast_fusion.10), channel_id=1, source_target_pairs={{0,8},{8,0},{1,9},{9,1},{2,10},{10,2},{3,11},{11,3},{4,12},{12,4},... | collective-permute-start | bytes 589832 | tf_op jit(solution)/shard_map/ppermute | solution.py:57
  163.7 5.8 %collective-permute-start.23 = (f32[192,256]{1,0:T(8,128)S(1)}, f32[192,256]{1,0:T(8,128)S(1)}, u32[]{:S(2)}, u32[]{:S(2)}) collective-permute-start(f32[192,256]{1,0:T(8,128)S(1)} %dynamic-slice_bitcast_fusion.9), channel_id=1, source_target_pairs={{0,8},{8,0},{1,9},{9,1},{2,10},{10,2},{3,11},{11,3},{4,12},{12,4},... | collective-permute-start | bytes 589832 | tf_op jit(solution)/shard_map/ppermute | solution.py:57
  165.9 4.3 %copy-start.4 = (f32[192,256]{1,0:T(8,128)}, f32[192,256]{1,0:T(8,128)S(1)}, u32[]{:S(2)}) copy-start(f32[192,256]{1,0:T(8,128)S(1)} %fusion.21) | copy-start | bytes 589828
  169.7 4.3 %copy-start.14 = (f32[192,256]{1,0:T(8,128)}, f32[192,256]{1,0:T(8,128)S(1)}, u32[]{:S(2)}) copy-start(f32[192,256]{1,0:T(8,128)S(1)} %fusion.17) | copy-start | bytes 589828
  170.3 3.6 %collective-permute-start.24 = (f32[384,256]{1,0:T(8,128)S(1)}, f32[384,256]{1,0:T(8,128)S(1)}, u32[]{:S(2)}, u32[]{:S(2)}) collective-permute-start(f32[384,256]{1,0:T(8,128)S(1)} %dynamic-slice_bitcast_fusion.2), channel_id=1, source_target_pairs={{0,1},{1,0},{2,3},{3,2},{4,5},{5,4},{6,7},{7,6},{8,9},{9,8},{10,11... | collective-permute-start | bytes 1179656 | tf_op jit(solution)/shard_map/ppermute | solution.py:64
  174.0 4.1 %collective-permute-start.25 = (f32[96,256]{1,0:T(8,128)S(1)}, f32[96,256]{1,0:T(8,128)S(1)}, u32[]{:S(2)}, u32[]{:S(2)}) collective-permute-start(f32[96,256]{1,0:T(8,128)S(1)} %get-tuple-element.68), channel_id=1, source_target_pairs={{0,2},{2,0},{4,6},{6,4},{1,3},{3,1},{5,7},{7,5},{8,10},{10,8},{12,... | collective-permute-start | bytes 294920 | tf_op jit(solution)/shard_map/ppermute | solution.py:66
  174.1 5.7 %collective-permute-start.26 = (f32[96,256]{1,0:T(8,128)S(1)}, f32[96,256]{1,0:T(8,128)S(1)}, u32[]{:S(2)}, u32[]{:S(2)}) collective-permute-start(f32[96,256]{1,0:T(8,128)S(1)} %get-tuple-element.67), channel_id=1, source_target_pairs={{0,4},{2,6},{4,0},{6,2},{1,5},{3,7},{5,1},{7,3},{8,12},{10,14},{12... | collective-permute-start | bytes 294920 | tf_op jit(solution)/shard_map/ppermute | solution.py:66
  175.2 7.5 %collective-permute-start.27 = (f32[96,256]{1,0:T(8,128)S(1)}, f32[96,256]{1,0:T(8,128)S(1)}, u32[]{:S(2)}, u32[]{:S(2)}) collective-permute-start(f32[96,256]{1,0:T(8,128)S(1)} %get-tuple-element.66), channel_id=1, source_target_pairs={{0,6},{2,4},{4,2},{6,0},{1,7},{3,5},{5,3},{7,1},{8,14},{10,12},{12... | collective-permute-start | bytes 294920 | tf_op jit(solution)/shard_map/ppermute | solution.py:66
  182.7 5.5 %collective-permute-start.29 = (f32[96,256]{1,0:T(8,128)S(1)}, f32[96,256]{1,0:T(8,128)S(1)}, u32[]{:S(2)}, u32[]{:S(2)}) collective-permute-start(f32[96,256]{1,0:T(8,128)S(1)} %fusion.22), channel_id=1, source_target_pairs={{0,64},{32,96},{64,0},{96,32},{1,65},{33,97},{65,1},{97,33},{2,66}... | collective-permute-start | bytes 294920 | tf_op jit(solution)/shard_map/ppermute | solution.py:68
  182.8 7.8 %collective-permute-start.30 = (f32[96,256]{1,0:T(8,128)S(1)}, f32[96,256]{1,0:T(8,128)S(1)}, u32[]{:S(2)}, u32[]{:S(2)}) collective-permute-start(f32[96,256]{1,0:T(8,128)S(1)} %fusion.22), channel_id=1, source_target_pairs={{0,96},{32,64},{64,32},{96,0},{1,97},{33,65},{65,33},{97,1},{2,98}... | collective-permute-start | bytes 294920 | tf_op jit(solution)/shard_map/ppermute | solution.py:68
  184.7 6.0 %collective-permute-start.28 = (f32[96,256]{1,0:T(8,128)S(1)}, f32[96,256]{1,0:T(8,128)S(1)}, u32[]{:S(2)}, u32[]{:S(2)}) collective-permute-start(f32[96,256]{1,0:T(8,128)S(1)} %fusion.22), channel_id=1, source_target_pairs={{0,32},{32,0},{64,96},{96,64},{1,33},{33,1},{65,97},{97,65},{2,34}... | collective-permute-start | bytes 294920 | tf_op jit(solution)/shard_map/ppermute | solution.py:68
  190.7 5.1 %collective-permute-start.32 = (f32[96,256]{1,0:T(8,128)S(1)}, f32[96,256]{1,0:T(8,128)S(1)}, u32[]{:S(2)}, u32[]{:S(2)}) collective-permute-start(f32[96,256]{1,0:T(8,128)S(1)} %add_add_fusion.1), channel_id=1, source_target_pairs={{0,16},{8,24},{16,0},{24,8},{1,17},{9,25},{17,1},{25,9},{2,18},{10... | collective-permute-start | bytes 294920 | tf_op jit(solution)/shard_map/ppermute | solution.py:70
  193.5 4.7 %collective-permute-start.33 = (f32[96,256]{1,0:T(8,128)S(1)}, f32[96,256]{1,0:T(8,128)S(1)}, u32[]{:S(2)}, u32[]{:S(2)}) collective-permute-start(f32[96,256]{1,0:T(8,128)S(1)} %add_add_fusion.1), channel_id=1, source_target_pairs={{0,24},{8,16},{16,8},{24,0},{1,25},{9,17},{17,9},{25,1},{2,26},{10... | collective-permute-start | bytes 294920 | tf_op jit(solution)/shard_map/ppermute | solution.py:70
  194.8 3.5 %collective-permute-start.31 = (f32[96,256]{1,0:T(8,128)S(1)}, f32[96,256]{1,0:T(8,128)S(1)}, u32[]{:S(2)}, u32[]{:S(2)}) collective-permute-start(f32[96,256]{1,0:T(8,128)S(1)} %add_add_fusion.1), channel_id=1, source_target_pairs={{0,8},{8,0},{16,24},{24,16},{1,9},{9,1},{17,25},{25,17},{2,10},{10... | collective-permute-start | bytes 294920 | tf_op jit(solution)/shard_map/ppermute | solution.py:70
  198.3 5.1 %collective-permute-start.36 = (f32[96,256]{1,0:T(8,128)S(1)}, f32[96,256]{1,0:T(8,128)S(1)}, u32[]{:S(2)}, u32[]{:S(2)}) collective-permute-start(f32[96,256]{1,0:T(8,128)S(1)} %add_add_fusion), channel_id=1, source_target_pairs={{0,6},{2,4},{4,2},{6,0},{1,7},{3,5},{5,3},{7,1},{8,14},{10,12},{12... | collective-permute-start | bytes 294920 | tf_op jit(solution)/shard_map/ppermute | solution.py:72
  200.8 5.1 %collective-permute-start.35 = (f32[96,256]{1,0:T(8,128)S(1)}, f32[96,256]{1,0:T(8,128)S(1)}, u32[]{:S(2)}, u32[]{:S(2)}) collective-permute-start(f32[96,256]{1,0:T(8,128)S(1)} %add_add_fusion), channel_id=1, source_target_pairs={{0,4},{2,6},{4,0},{6,2},{1,5},{3,7},{5,1},{7,3},{8,12},{10,14},{12... | collective-permute-start | bytes 294920 | tf_op jit(solution)/shard_map/ppermute | solution.py:72
  200.8 5.1 %collective-permute-start.34 = (f32[96,256]{1,0:T(8,128)S(1)}, f32[96,256]{1,0:T(8,128)S(1)}, u32[]{:S(2)}, u32[]{:S(2)}) collective-permute-start(f32[96,256]{1,0:T(8,128)S(1)} %add_add_fusion), channel_id=1, source_target_pairs={{0,2},{2,0},{4,6},{6,4},{1,3},{3,1},{5,7},{7,5},{8,10},{10,8},{12,... | collective-permute-start | bytes 294920 | tf_op jit(solution)/shard_map/ppermute | solution.py:72
  206.0 5.2 %collective-permute-start.37 = (f32[384,256]{1,0:T(8,128)S(1)}, f32[384,256]{1,0:T(8,128)S(1)}, u32[]{:S(2)}, u32[]{:S(2)}) collective-permute-start(f32[384,256]{1,0:T(8,128)S(1)} %pad_maximum_fusion.6), channel_id=1, source_target_pairs={{0,1},{1,0},{2,3},{3,2},{4,5},{5,4},{6,7},{7,6},{8,9},{9,8},{10,11... | collective-permute-start | bytes 1179656 | tf_op jit(solution)/shard_map/ppermute | solution.py:76
  211.3 1.0 copy-start.17
  211.3 1.2 copy-start.18
  212.3 1.4 copy-start.8
  212.6 1.1 copy-start.9

commit v2 on v0

v2 whole, which is shorter than its diff:
```python
import jax
import jax.numpy as jnp
from jax import lax
from jax.experimental import pallas as pl
from jax.experimental.pallas import tpu as pltpu
from jax.sharding import Mesh, PartitionSpec as P

BLK = 128
AXES = ("y", "zh", "zl", "x", "c")
RING_UP = [(i, (i + 1) % 4) for i in range(4)]
RING_DOWN = [(i, (i + 3) % 4) for i in range(4)]
SWAP = [(0, 1), (1, 0)]


def flip(bits, size):
    return [(i, i ^ bits) for i in range(size)]


def matmul(left, right):
    return jnp.dot(left, right, precision=lax.Precision.HIGH, preferred_element_type=jnp.float32)


def spread_pairs():
    pairs = []
    for source in range(128):
        y, zh, zl, x, c = source >> 5, source >> 4 & 1, source >> 3 & 1, source >> 1 & 3, source & 1
        target = ((x + y) % 4, c, y >> 1, (y & 1) * 2 + zh, zl)
        pairs.append((source, ((((target[0] * 2 + target[1]) * 2 + target[2]) * 4 + target[3]) * 2 + target[4])))
    return pairs


def split(value):
    high = value.astype(jnp.bfloat16)
    return high, (value - high.astype(jnp.float32)).astype(jnp.bfloat16)


def product_kernel(other_core, inverse, rows, out, right_high, right_low, buffers, sems):
    y, _, zl, x, c = [lax.axis_index(name) for name in AXES]
    core = 1 - c if other_core else c
    chunks, size, _ = out.shape
    steps = chunks // 2
    slots = buffers.shape[0]

    def copies(t):
        slot = t % slots
        starts = [pl.multiple_of(((zl ^ side) * 8 + (x + t) % 4 * 2 + core) * size, 64) for side in range(2)]
        return [
            pltpu.make_async_copy(
                inverse.at[pl.ds(start, size)], buffers.at[slot, pl.ds(side * size, size)], sems.at[slot, side]
            )
            for side, start in enumerate(starts)
        ]

    for t in range(slots):
        for copy in copies(t):
            copy.start()

    shift = (y - (zl * 2 + x // 2) + 4) % 4
    group_rows = rows.shape[0] // 4
    for offset in range(4):
        start = pl.multiple_of((offset + shift) % 4 * group_rows, BLK)
        high, low = split(rows[offset * group_rows : (offset + 1) * group_rows, :])
        right_high[pl.ds(start, group_rows), :] = high
        right_low[pl.ds(start, group_rows), :] = low

    def step(t, carry):
        for copy in copies(t):
            copy.wait()
        high, low = split(buffers[t % slots])
        dot = lambda a, b: jnp.dot(a, b, preferred_element_type=jnp.float32)
        total = dot(high, right_high[...]) + (dot(high, right_low[...]) + dot(low, right_high[...]))
        out[2 * t] = total[:size]
        out[2 * t + 1] = total[size:]

        @pl.when(t + slots < steps)
        def _():
            for copy in copies(t + slots):
                copy.start()

        return carry

    lax.fori_loop(0, steps, step, 0)


def block_product(inverse, rows, other_core):
    size = inverse.shape[0] // 16
    width = rows.shape[1]
    slots = 3
    whole = pl.BlockSpec(memory_space=pltpu.VMEM)
    return pl.pallas_call(
        lambda *refs: product_kernel(other_core, *refs),
        out_shape=jax.ShapeDtypeStruct((8, size, width), jnp.float32),
        in_specs=[pl.BlockSpec(memory_space=pltpu.HBM), whole],
        out_specs=whole,
        scratch_shapes=[
            pltpu.VMEM(rows.shape, jnp.bfloat16),
            pltpu.VMEM(rows.shape, jnp.bfloat16),
            pltpu.VMEM((slots, 2 * size, inverse.shape[1]), jnp.float32),
            pltpu.SemaphoreType.DMA((slots, 2)),
        ],
        compiler_params=pltpu.CompilerParams(vmem_limit_bytes=46 * 1024 * 1024),
        cost_estimate=pl.CostEstimate(flops=6 * size * 8 * inverse.shape[1] * width, bytes_accessed=inverse.size * 2, transcendentals=0),
        name="send_product" if other_core else "keep_product",
    )(inverse, rows)


def combine_kernel(keep, got, own_rows, zl_rows, down_rows, low_rows, high_rows, up_rows,
                   mine, far_low, far_high, near_up, near_down, products, sums):
    x, c = lax.axis_index("x"), lax.axis_index("c")
    _, size, both = keep.shape
    width = both // 2
    half = size // 2
    sums[...] = jnp.zeros_like(sums)

    def chunk(offset, side):
        total = keep[2 * offset + side] + got[2 * offset + side]
        if offset == 0:
            rows = (own_rows, zl_rows)[side][...]
            mine[side] = total
        elif offset == 1:
            rows = down_rows[side]
            near_up[side] = total
        elif offset == 2:
            rows = (low_rows, high_rows)[side][...]
            far_low[side] = total[:half]
            far_high[side] = total[half:]
        else:
            rows = up_rows[side]
            near_down[side] = total
        return total, rows

    for offset in range(4):
        totals, rows = zip(*[chunk(offset, side) for side in range(2)])
        image_high, image_low = split(jnp.concatenate(totals))
        rows_high, rows_low = split(jnp.concatenate(rows))
        across = (((0,), (0,)), ((), ()))
        dot = lambda a, b: lax.dot_general(a, b, across, preferred_element_type=jnp.float32)
        product = lambda ah, al, bh, bl: dot(ah, bh) + (dot(ah, bl) + dot(al, bh))
        sums[: 2 * width] += product(rows_high, rows_low, image_high[:, :width], image_low[:, :width])
        sums[2 * width :] += product(
            rows_high[:, width:], rows_low[:, width:], image_high[:, width:], image_low[:, width:]
        )
    part = sums.shape[0] // 8
    for dc in range(2):
        for dx in range(4):
            start = pl.multiple_of(((c ^ dc) * 4 + (x ^ dx)) * part, 8)
            products[dc, dx] = sums[pl.ds(start, part), :]


def combine(keep, got, pieces):
    _, size, both = keep.shape
    width = both // 2
    part = jax.ShapeDtypeStruct((2, size, both), jnp.float32)
    half = jax.ShapeDtypeStruct((2, size // 2, both), jnp.float32)
    products = jax.ShapeDtypeStruct((2, 4, 3 * width // 8, width), jnp.float32)
    whole = pl.BlockSpec(memory_space=pltpu.VMEM)
    return pl.pallas_call(
        combine_kernel,
        out_shape=(part, half, half, part, part, products),
        in_specs=[whole] * 8,
        out_specs=[whole] * 6,
        scratch_shapes=[pltpu.VMEM((3 * width, width), jnp.float32)],
        compiler_params=pltpu.CompilerParams(vmem_limit_bytes=24 * 1024 * 1024),
        cost_estimate=pl.CostEstimate(flops=18 * 8 * size * width * width, bytes_accessed=keep.size * 16, transcendentals=0),
        name="combine",
    )(keep, got, *pieces)


def finish_kernel(own, other, child_top, diag_parent, diag_child, parent_diagonal, child_upper, child_diagonal, sums):
    x, c = lax.axis_index("x"), lax.axis_index("c")
    part = own.shape[1]
    width = child_top.shape[0]
    for dc, source in enumerate((own, other)):
        for dx in range(4):
            start = pl.multiple_of(((c ^ dc) * 4 + (x ^ dx)) * part, 8)
            sums[pl.ds(start, part), :] = source[dx]

    def dot(a, b, dims=(((1,), (0,)), ((), ()))):
        return lax.dot_general(a, b, dims, precision=lax.Precision.HIGHEST, preferred_element_type=jnp.float32)

    top = child_top[...]
    cross = sums[width : 2 * width]
    diagonal = diag_parent[...] + sums[:width]
    parent_diagonal[...] = diagonal
    upper = cross.T - dot(diagonal, top)
    child_upper[...] = upper
    inner = dot(top, upper, (((0,), (0,)), ((), ()))) + dot(cross, top)
    child_diagonal[...] = diag_child[...] - inner + sums[2 * width :]


def finish(own, other, child_top, diag_parent, diag_child):
    whole = pl.BlockSpec(memory_space=pltpu.VMEM)
    block = jax.ShapeDtypeStruct(child_top.shape, jnp.float32)
    return pl.pallas_call(
        finish_kernel,
        out_shape=(block, block, block),
        in_specs=[whole] * 5,
        out_specs=[whole] * 3,
        scratch_shapes=[pltpu.VMEM((3 * child_top.shape[0], child_top.shape[1]), jnp.float32)],
        compiler_params=pltpu.CompilerParams(vmem_limit_bytes=16 * 1024 * 1024),
        name="finish",
    )(own, other, child_top, diag_parent, diag_child)


def sum_all(products):
    own = products[0] + lax.ppermute(products[1], "c", SWAP)
    got = [lax.ppermute(own[bits], "x", flip(bits, 4)) for bits in (1, 2, 3)]
    own = (own[0] + got[0]) + (got[1] + got[2])
    got = [lax.ppermute(own, "y", flip(bits, 4)) for bits in (1, 2, 3)]
    own = (own + got[0]) + (got[1] + got[2])
    got = [lax.ppermute(own, ("zh", "zl"), flip(bits, 4)) for bits in (1, 2, 3)]
    own = (own + got[0]) + (got[1] + got[2])
    own = jnp.stack([own] + [lax.ppermute(own, "x", flip(bits, 4)) for bits in (1, 2, 3)])
    return own, lax.ppermute(own, "c", SWAP)


def images_of(masked, inverse, zh):
    rows, _ = masked.shape
    spread = lax.ppermute(masked, AXES, spread_pairs())
    other = lax.ppermute(spread, "zh", SWAP)
    pair = jnp.where(zh == 0, jnp.concatenate([spread, other]), jnp.concatenate([other, spread]))
    up = lax.ppermute(pair, "y", RING_UP)
    down = lax.ppermute(pair, "y", RING_DOWN)
    low = lax.ppermute(up[:rows], "y", RING_UP)
    high = lax.ppermute(down[rows:], "y", RING_DOWN)
    gathered = jnp.concatenate([pair, down, low, high, up])
    row_side = lax.ppermute(masked, "zl", SWAP)
    row_pair = jnp.stack([masked, row_side])
    row_up = lax.ppermute(row_pair, "x", RING_UP)
    row_down = lax.ppermute(row_pair, "x", RING_DOWN)
    row_low = lax.ppermute(row_up[0], "x", RING_UP)
    row_high = lax.ppermute(row_down[1], "x", RING_DOWN)
    send = block_product(inverse, gathered, True)
    keep = block_product(inverse, gathered, False)
    got = lax.ppermute(send, "c", SWAP)
    mine, far_low, far_high, near_up, near_down, products = combine(
        keep, got, (masked, row_side, row_down, row_low, row_high, row_up)
    )
    half = rows // 2
    far_low = lax.ppermute(far_low, "x", RING_UP)
    far_high = lax.ppermute(far_high, "x", RING_DOWN)
    from_low = jnp.concatenate([near_up[:, :half] + far_low, near_up[:, half:]], axis=1)
    from_high = jnp.concatenate([near_down[:, :half], near_down[:, half:] + far_high], axis=1)
    from_low = lax.ppermute(from_low, "x", RING_UP)
    from_high = lax.ppermute(from_high, "x", RING_DOWN)
    last = lax.ppermute(mine[1] + from_low[1] + from_high[1], "zl", SWAP)
    return mine[0] + from_low[0] + from_high[0] + last, products


def local_mask(blocks, device, rows):
    block = (device * rows + lax.broadcasted_iota(jnp.int32, (rows, blocks.shape[0]), 0)) // BLK
    chosen = block == lax.broadcasted_iota(jnp.int32, (rows, blocks.shape[0]), 1)
    return jnp.sum(jnp.where(chosen, blocks[None, :].astype(jnp.float32), 0.0), axis=1, keepdims=True)


def local_step(inverse, parent_panel, child_panel, child_top, diag_parent, diag_child, parent_blocks, child_blocks):
    y, zh, zl, x, c = [lax.axis_index(name) for name in AXES]
    device = (((y * 2 + zh) * 2 + zl) * 4 + x) * 2 + c
    rows = parent_panel.shape[0]
    parent_mask = local_mask(parent_blocks, device, rows)
    child_mask = local_mask(child_blocks, device, rows)
    masked = jnp.concatenate([parent_panel * parent_mask, child_panel * child_mask], axis=1)
    images, products = images_of(masked, inverse, zh)
    width = parent_panel.shape[1]
    parent_column = -(parent_mask * images[:, :width])
    child_column = -(child_mask * (matmul(parent_column, child_top) + images[:, width:]))
    parent_diagonal, child_upper, child_diagonal = finish(*sum_all(products), child_top, diag_parent, diag_child)
    return parent_column, parent_diagonal, child_column, child_upper, child_diagonal


def solution(mesh):
    fine = Mesh(mesh.devices.reshape(4, 2, 2, 4, 2), AXES)
    everywhere = P(AXES, None)
    whole = P(None, None)
    return jax.shard_map(
        local_step,
        mesh=fine,
        in_specs=(P(("y", "zh"), ("zl", "x", "c")), everywhere, everywhere, whole, whole, whole, P(None), P(None)),
        out_specs=(everywhere, whole, everywhere, whole, whole),
        check_vma=False,
    )
```

time: 558 us -> 191 us (0.34)
  waiting for transfers between devices: 356 us -> 93.7 us
  matrix products: 49.4 us -> 0.94 us
  blocking collectives: 29.3 us -> 0 us
  local copies, waits for them, and re-layouts: 29.3 us -> 0.35 us
  Pallas kernels: 0 us -> 24.1 us
  between operations: 20.5 us -> 0.98 us
  other arithmetic: 16.9 us -> 5.57 us
  starting transfers between devices: 55.9 us -> 65.4 us
    dot_general x1 -> x0, waiting for transfers between devices: 150 us -> none  [matmul(): jnp.dot(left, right, precision=lax.Precision.HIGHEST, preferred_element_t...]
    unnamed x16 -> x0, waiting for transfers between devices: 120 us -> none
    ppermute x0 -> x31, waiting for transfers between devices: none -> 93.7 us  [the longest x1 16.5 us: images_of(): up = lax.ppermute(pair, 'y', RING_UP)]
    mul x4 -> x0, waiting for transfers between devices: 85.8 us -> none  [the longest x2 46 us: reference(): parent_masked = parent_panel * parent_mask]
    ppermute x0 -> x31, starting transfers between devices: none -> 65.4 us  [the longest x1 8.88 us: images_of(): up = lax.ppermute(pair, 'y', RING_UP)]
    dot_general x8 -> x1, matrix products: 49.4 us -> 0.94 us  [matmul(): jnp.dot(left, right, precision=lax.Precision.HIGH, preferred_element_type...]
    mul x4 -> x0, starting transfers between devices: 34.5 us -> none  [the longest x2 28.5 us: reference(): parent_masked = parent_panel * parent_mask]
    unnamed x2 -> x0, blocking collectives: 29.3 us -> none
  transfers between devices with their start and end apart: 16 -> 31, of which waited for: 11 -> 15; matrix products, arithmetic and copies ran while one was open for 11% -> 0% of each run, Pallas kernels for 0% -> 6%
where the time goes in v2:
time: 191 us
  waiting for transfers between devices  93.7 us (49%)
  starting transfers between devices  65.4 us (34%)
  Pallas kernels  24.1 us (13%)
  other arithmetic  5.57 us (3%)
    pallas_call x2, Pallas kernels, block_product(): pl.pallas_call(lambda *refs: product_kernel(other_core, *refs), out_shape...  19.5 us
    ppermute x1, waiting for transfers between devices, images_of(): up = lax.ppermute(pair, 'y', RING_UP)  16.5 us
    ppermute x1, waiting for transfers between devices, images_of(): row_up = lax.ppermute(row_pair, 'x', RING_UP)  16.2 us
    ppermute x1, waiting for transfers between devices, images_of(): row_side = lax.ppermute(masked, 'zl', SWAP)  10.6 us
    ppermute x1, waiting for transfers between devices, images_of(): other = lax.ppermute(spread, 'zh', SWAP)  10.3 us
    ppermute x1, starting transfers between devices, images_of(): up = lax.ppermute(pair, 'y', RING_UP)  8.88 us
    ppermute x1, waiting for transfers between devices, images_of(): last = lax.ppermute(mine[1] + from_low[1] + from_high[1], 'zl', SWAP)  7.56 us
    ppermute x1, waiting for transfers between devices, images_of(): low = lax.ppermute(up[:rows], 'y', RING_UP)  7.18 us
  transfers between devices with their start and end apart: 31, of which 15 were waited for; matrix products, arithmetic and copies ran while one was open for 0% of the time, Pallas kernels for 6%

profile of v2, /device:TPU:1, one launch (start us, length us, event | category | flops | bytes accessed | tf_op | source)
XLA Modules:
  0.0 191.0 jit_solution(15409873391407136121)
XLA Ops:
  0.7 0.7 convert_element_type.8
  1.4 0.7 convert_element_type.9
  2.0 0.3 select_reduce_fusion.1
  2.3 1.0 broadcast_multiply_fusion.1
  3.3 1.0 broadcast_multiply_fusion
  4.4 0.8 fusion.9
  5.2 6.9 %collective-permute-start = (f32[192,512]{1,0:T(8,128)S(1)}, f32[192,512]{1,0:T(8,128)S(1)}, u32[]{:S(2)}, u32[]{:S(2)}) collective-permute-start(f32[192,512]{1,0:T(8,128)S(1)} %get-tuple-element.35.own_rows), channel_id=1, source_target_pairs={{0,0},{1,16},{2,32},{3,48},{4,64},{5,80},{6,96},{7,112},{8,1},{9,1... | collective-permute-start | bytes 1179656 | tf_op jit(solution)/shard_map/ppermute | solution.py:219
  12.1 5.4 %collective-permute-done = f32[192,512]{1,0:T(8,128)S(1)} collective-permute-done((f32[192,512]{1,0:T(8,128)S(1)}, f32[192,512]{1,0:T(8,128)S(1)}, u32[]{:S(2)}, u32[]{:S(2)}) %collective-permute-start) | collective-permute-done | bytes 393248 | tf_op jit(solution)/shard_map/ppermute | solution.py:219
  17.5 4.9 %collective-permute-start.1 = (f32[192,512]{1,0:T(8,128)S(1)}, f32[192,512]{1,0:T(8,128)S(1)}, u32[]{:S(2)}, u32[]{:S(2)}) collective-permute-start(f32[192,512]{1,0:T(8,128)S(1)} %collective-permute-done), channel_id=1, source_target_pairs={{0,16},{16,0},{1,17},{17,1},{2,18},{18,2},{3,19},{19,3},{4,20},{20... | collective-permute-start | bytes 1179656 | tf_op jit(solution)/shard_map/ppermute | solution.py:220
  22.4 10.3 %collective-permute-done.1 = f32[192,512]{1,0:T(8,128)S(1)} collective-permute-done((f32[192,512]{1,0:T(8,128)S(1)}, f32[192,512]{1,0:T(8,128)S(1)}, u32[]{:S(2)}, u32[]{:S(2)}) %collective-permute-start.1) | collective-permute-done | bytes 393248 | tf_op jit(solution)/shard_map/ppermute | solution.py:220
  32.7 0.2 constant_dynamic-update-slice_fusion.4
  32.9 8.9 %collective-permute-start.3 = (f32[384,512]{1,0:T(8,128)S(1)}, f32[384,512]{1,0:T(8,128)S(1)}, u32[]{:S(2)}, u32[]{:S(2)}) collective-permute-start(f32[384,512]{1,0:T(8,128)S(1)} %get-tuple-element.26), channel_id=1, source_target_pairs={{0,32},{32,64},{64,96},{96,0},{1,33},{33,65},{65,97},{97,1},{2,34}... | collective-permute-start | bytes 2359304 | tf_op jit(solution)/shard_map/ppermute | solution.py:222
  41.8 4.7 %collective-permute-start.2 = (f32[384,512]{1,0:T(8,128)S(1)}, f32[384,512]{1,0:T(8,128)S(1)}, u32[]{:S(2)}, u32[]{:S(2)}) collective-permute-start(f32[384,512]{1,0:T(8,128)S(1)} %get-tuple-element.26), channel_id=1, source_target_pairs={{0,96},{32,0},{64,32},{96,64},{1,97},{33,1},{65,33},{97,65},{2,98}... | collective-permute-start | bytes 2359304 | tf_op jit(solution)/shard_map/ppermute | solution.py:223
  46.5 16.5 %collective-permute-done.3 = f32[384,512]{1,0:T(8,128)S(1)} collective-permute-done((f32[384,512]{1,0:T(8,128)S(1)}, f32[384,512]{1,0:T(8,128)S(1)}, u32[]{:S(2)}, u32[]{:S(2)}) %collective-permute-start.3) | collective-permute-done | bytes 786464 | tf_op jit(solution)/shard_map/ppermute | solution.py:222
  63.0 0.1 collective-permute-start.4
  63.2 2.7 %collective-permute-start.5 = (f32[192,512]{1,0:T(8,128)S(1)}, f32[192,512]{1,0:T(8,128)S(1)}, u32[]{:S(2)}, u32[]{:S(2)}) collective-permute-start(f32[192,512]{1,0:T(8,128)S(1)} %slice.89), channel_id=1, source_target_pairs={{0,96},{32,0},{64,32},{96,64},{1,97},{33,1},{65,33},{97,65},{2,98}... | collective-permute-start | bytes 1179656 | tf_op jit(solution)/shard_map/ppermute | solution.py:225
  65.9 0.1 constant_dynamic-update-slice_fusion.3
  65.9 7.2 %collective-permute-done.4 = f32[192,512]{1,0:T(8,128)S(1)} collective-permute-done((f32[192,512]{1,0:T(8,128)S(1)}, f32[192,512]{1,0:T(8,128)S(1)}, u32[]{:S(2)}, u32[]{:S(2)}) %collective-permute-start.4) | collective-permute-done | bytes 393248 | tf_op jit(solution)/shard_map/ppermute | solution.py:224
  73.2 0.1 constant_dynamic-update-slice_fusion.refs_1_
  73.3 9.8 %send_product.1 = f32[8,192,512]{2,1,0:T(8,128)S(1)} custom-call(f32[3072,1536]{1,0:T(8,128)} %refs_0_.3, f32[1536,512]{1,0:T(8,128)S(1)} %constant_dynamic-update-slice_fusion.refs_1_), custom_call_target="tpu_custom_call" | custom-call | flops 7247757312 | bytes 9437184 | tf_op jit(solution)/shard_map/send_product/pallas_call | solution.py:90
  83.0 2.8 %collective-permute-start.6 = (f32[8,192,512]{2,1,0:T(8,128)S(1)}, f32[8,192,512]{2,1,0:T(8,128)S(1)}, u32[]{:S(2)}, u32[]{:S(2)}) collective-permute-start(f32[8,192,512]{2,1,0:T(8,128)S(1)} %send_product.1), channel_id=1, source_target_pairs={{0,1},{1,0},{2,3},{3,2},{4,5},{5,4},{6,7},{7,6},{8,9},{9,8},{10,11... | collective-permute-start | bytes 9437192 | tf_op jit(solution)/shard_map/ppermute | solution.py:235
  85.9 10.6 %collective-permute-done.7.zl_rows = f32[192,512]{1,0:T(8,128)S(1)} collective-permute-done((f32[192,512]{1,0:T(8,128)S(1)}, f32[192,512]{1,0:T(8,128)S(1)}, u32[]{:S(2)}, u32[]{:S(2)}) %collective-permute-start.7) | collective-permute-done | bytes 393248 | tf_op jit(solution)/shard_map/ppermute | solution.py:227
  96.4 0.1 pad_maximum_fusion
  96.5 3.2 %collective-permute-start.9 = (f32[2,192,512]{2,1,0:T(8,128)S(1)}, f32[2,192,512]{2,1,0:T(8,128)S(1)}, u32[]{:S(2)}, u32[]{:S(2)}) collective-permute-start(f32[2,192,512]{2,1,0:T(8,128)S(1)} %pad_maximum_fusion), channel_id=1, source_target_pairs={{0,2},{2,4},{4,6},{6,0},{1,3},{3,5},{5,7},{7,1},{8,10},{10,12},{12... | collective-permute-start | bytes 2359304 | tf_op jit(solution)/shard_map/ppermute | solution.py:229
  99.7 16.2 %collective-permute-done.9.up_rows = f32[2,192,512]{2,1,0:T(8,128)S(1)} collective-permute-done((f32[2,192,512]{2,1,0:T(8,128)S(1)}, f32[2,192,512]{2,1,0:T(8,128)S(1)}, u32[]{:S(2)}, u32[]{:S(2)}) %collective-permute-start.9) | collective-permute-done | bytes 786464 | tf_op jit(solution)/shard_map/ppermute | solution.py:229
  116.0 2.2 %collective-permute-start.10 = (f32[192,512]{1,0:T(8,128)S(1)}, f32[192,512]{1,0:T(8,128)S(1)}, u32[]{:S(2)}, u32[]{:S(2)}) collective-permute-start(f32[192,512]{1,0:T(8,128)S(1)} %slice_bitcast_fusion.1), channel_id=1, source_target_pairs={{0,2},{2,4},{4,6},{6,0},{1,3},{3,5},{5,7},{7,1},{8,10},{10,12},{12... | collective-permute-start | bytes 1179656 | tf_op jit(solution)/shard_map/ppermute | solution.py:231
  118.2 1.1 collective-permute-start.11
  119.3 9.7 %keep_product.1.keep = f32[8,192,512]{2,1,0:T(8,128)S(1)} custom-call(f32[3072,1536]{1,0:T(8,128)} %refs_0_.3, f32[1536,512]{1,0:T(8,128)S(1)} %constant_dynamic-update-slice_fusion.refs_1_), custom_call_target="tpu_custom_call" | custom-call | flops 7247757312 | bytes 9437184 | tf_op jit(solution)/shard_map/keep_product/pallas_call | solution.py:90
  129.0 2.7 %combine.1 = (f32[2,192,512]{2,1,0:T(8,128)S(1)}, f32[2,96,512]{2,1,0:T(8,128)S(1)}, f32[2,96,512]{2,1,0:T(8,128)S(1)}, f32[2,192,512]{2,1,0:T(8,128)S(1)}, f32[...) custom-call(f32[8,192,512]{2,1,0:T(8,128)S(1)} %keep_product.1.keep, ...), custom_call_target="tpu_custom_call" | custom-call | flops 1811939328 | bytes 12582912 | tf_op jit(solution)/shard_map/combine/pallas_call | solution.py:157
  131.8 2.0 %collective-permute-start.17 = (f32[4,96,256]{2,1,0:T(8,128)S(1)}, f32[4,96,256]{2,1,0:T(8,128)S(1)}, u32[]{:S(2)}, u32[]{:S(2)}) collective-permute-start(f32[4,96,256]{2,1,0:T(8,128)S(1)} %slice_bitcast_fusion.2), channel_id=1, source_target_pairs={{0,1},{1,0},{2,3},{3,2},{4,5},{5,4},{6,7},{7,6},{8,9},{9,8},{10,11... | collective-permute-start | bytes 1179656 | tf_op jit(solution)/shard_map/ppermute | solution.py:206
  133.8 0.6 collective-permute-start.12
  134.5 2.0 %collective-permute-start.14 = (f32[2,96,512]{2,1,0:T(8,128)S(1)}, f32[2,96,512]{2,1,0:T(8,128)S(1)}, u32[]{:S(2)}, u32[]{:S(2)}) collective-permute-start(f32[2,96,512]{2,1,0:T(8,128)S(1)} %get-tuple-element.18), channel_id=1, source_target_pairs={{0,6},{2,0},{4,2},{6,4},{1,7},{3,1},{5,3},{7,5},{8,14},{10,8},{12,... | collective-permute-start | bytes 1179656 | tf_op jit(solution)/shard_map/ppermute | solution.py:241
  136.5 0.1 bitcast_add_fusion
  136.6 0.3 collective-permute-start.20
  136.9 1.2 collective-permute-start.19
  138.1 2.0 %collective-permute-start.18 = (f32[96,256]{1,0:T(8,128)S(1)}, f32[96,256]{1,0:T(8,128)S(1)}, u32[]{:S(2)}, u32[]{:S(2)}) collective-permute-start(f32[96,256]{1,0:T(8,128)S(1)} %get-tuple-element.33), channel_id=1, source_target_pairs={{0,2},{2,0},{4,6},{6,4},{1,3},{3,1},{5,7},{7,5},{8,10},{10,8},{12,... | collective-permute-start | bytes 294920 | tf_op jit(solution)/shard_map/ppermute | solution.py:207
  140.1 4.9 %collective-permute-done.14 = f32[2,96,512]{2,1,0:T(8,128)S(1)} collective-permute-done((f32[2,96,512]{2,1,0:T(8,128)S(1)}, f32[2,96,512]{2,1,0:T(8,128)S(1)}, u32[]{:S(2)}, u32[]{:S(2)}) %collective-permute-start.14) | collective-permute-done | bytes 393248 | tf_op jit(solution)/shard_map/ppermute | solution.py:241
  145.0 0.1 fusion.10
  145.1 0.1 pad_maximum_fusion.2
  145.1 4.0 %collective-permute-start.15 = (f32[2,192,512]{2,1,0:T(8,128)S(1)}, f32[2,192,512]{2,1,0:T(8,128)S(1)}, u32[]{:S(2)}, u32[]{:S(2)}) collective-permute-start(f32[2,192,512]{2,1,0:T(8,128)S(1)} %pad_maximum_fusion.2), channel_id=1, source_target_pairs={{0,6},{2,0},{4,2},{6,4},{1,7},{3,1},{5,3},{7,5},{8,14},{10,8},{12,... | collective-permute-start | bytes 2359304 | tf_op jit(solution)/shard_map/ppermute | solution.py:245
  149.1 0.1 slice_add_fusion.5
  149.2 0.6 collective-permute-done.20
  149.9 2.8 %collective-permute-start.23 = (f32[96,256]{1,0:T(8,128)S(1)}, f32[96,256]{1,0:T(8,128)S(1)}, u32[]{:S(2)}, u32[]{:S(2)}) collective-permute-start(f32[96,256]{1,0:T(8,128)S(1)} %fusion.7), channel_id=1, source_target_pairs={{0,96},{32,64},{64,32},{96,0},{1,97},{33,65},{65,33},{97,1},{2,98}... | collective-permute-start | bytes 294920 | tf_op jit(solution)/shard_map/ppermute | solution.py:209
  152.7 0.7 collective-permute-start.21
  153.4 0.1 collective-permute-start.13
  153.5 1.8 collective-permute-done.23
  155.3 2.4 %collective-permute-done.22 = f32[96,256]{1,0:T(8,128)S(1)} collective-permute-done((f32[96,256]{1,0:T(8,128)S(1)}, f32[96,256]{1,0:T(8,128)S(1)}, u32[]{:S(2)}, u32[]{:S(2)}) %collective-permute-start.22) | collective-permute-done | bytes 98336 | tf_op jit(solution)/shard_map/ppermute | solution.py:209
  157.8 2.1 %collective-permute-start.26 = (f32[96,256]{1,0:T(8,128)S(1)}, f32[96,256]{1,0:T(8,128)S(1)}, u32[]{:S(2)}, u32[]{:S(2)}) collective-permute-start(f32[96,256]{1,0:T(8,128)S(1)} %add_add_fusion.1), channel_id=1, source_target_pairs={{0,24},{8,16},{16,8},{24,0},{1,25},{9,17},{17,9},{25,1},{2,26},{10... | collective-permute-start | bytes 294920 | tf_op jit(solution)/shard_map/ppermute | solution.py:211
  159.9 1.0 collective-permute-start.25
  160.8 0.3 collective-permute-start.24
  161.1 1.7 collective-permute-done.26
  162.8 2.0 %collective-permute-done.25 = f32[96,256]{1,0:T(8,128)S(1)} collective-permute-done((f32[96,256]{1,0:T(8,128)S(1)}, f32[96,256]{1,0:T(8,128)S(1)}, u32[]{:S(2)}, u32[]{:S(2)}) %collective-permute-start.25) | collective-permute-done | bytes 98336 | tf_op jit(solution)/shard_map/ppermute | solution.py:211
  164.9 2.2 %collective-permute-start.29 = (f32[96,256]{1,0:T(8,128)S(1)}, f32[96,256]{1,0:T(8,128)S(1)}, u32[]{:S(2)}, u32[]{:S(2)}) collective-permute-start(f32[96,256]{1,0:T(8,128)S(1)} %add_add_fusion), channel_id=1, source_target_pairs={{0,6},{2,4},{4,2},{6,0},{1,7},{3,5},{5,3},{7,1},{8,14},{10,12},{12... | collective-permute-start | bytes 294920 | tf_op jit(solution)/shard_map/ppermute | solution.py:213
  167.0 1.2 collective-permute-start.27
  168.2 4.0 %collective-permute-done.29 = f32[96,256]{1,0:T(8,128)S(1)} collective-permute-done((f32[96,256]{1,0:T(8,128)S(1)}, f32[96,256]{1,0:T(8,128)S(1)}, u32[]{:S(2)}, u32[]{:S(2)}) %collective-permute-start.29) | collective-permute-done | bytes 98336 | tf_op jit(solution)/shard_map/ppermute | solution.py:213
  172.2 2.3 %collective-permute-done.28 = f32[96,256]{1,0:T(8,128)S(1)} collective-permute-done((f32[96,256]{1,0:T(8,128)S(1)}, f32[96,256]{1,0:T(8,128)S(1)}, u32[]{:S(2)}, u32[]{:S(2)}) %collective-permute-start.28) | collective-permute-done | bytes 98336 | tf_op jit(solution)/shard_map/ppermute | solution.py:213
  174.6 4.4 %collective-permute-start.30 = (f32[4,96,256]{2,1,0:T(8,128)S(1)}, f32[4,96,256]{2,1,0:T(8,128)S(1)}, u32[]{:S(2)}, u32[]{:S(2)}) collective-permute-start(f32[4,96,256]{2,1,0:T(8,128)S(1)} %pad_maximum_fusion.4.own), channel_id=1, source_target_pairs={{0,1},{1,0},{2,3},{3,2},{4,5},{5,4},{6,7},{7,6},{8,9},{9,8},{10,11... | collective-permute-start | bytes 1179656 | tf_op jit(solution)/shard_map/ppermute | solution.py:214
  179.0 0.1 fusion.2
  179.1 1.3 collective-permute-start.16
  180.4 1.9 finish.1
  182.3 7.6 %collective-permute-done.16 = f32[192,512]{1,0:T(8,128)S(1)} collective-permute-done((f32[192,512]{1,0:T(8,128)S(1)}, f32[192,512]{1,0:T(8,128)S(1)}, u32[]{:S(2)}, u32[]{:S(2)}) %collective-permute-start.16) | collective-permute-done | bytes 393248 | tf_op jit(solution)/shard_map/ppermute | solution.py:246
  189.8 0.1 fusion.4
  190.0 0.1 fusion.5
  190.1 0.9 fusion.1
  (45 shorter events, 0.5 us)
Async XLA Ops:
  5.2 12.3 %collective-permute-start = (f32[192,512]{1,0:T(8,128)S(1)}, f32[192,512]{1,0:T(8,128)S(1)}, u32[]{:S(2)}, u32[]{:S(2)}) collective-permute-start(f32[192,512]{1,0:T(8,128)S(1)} %get-tuple-element.35.own_rows), channel_id=1, source_target_pairs={{0,0},{1,16},{2,32},{3,48},{4,64},{5,80},{6,96},{7,112},{8,1},{9,1... | collective-permute-start | bytes 1179656 | tf_op jit(solution)/shard_map/ppermute | solution.py:219
  17.5 15.2 %collective-permute-start.1 = (f32[192,512]{1,0:T(8,128)S(1)}, f32[192,512]{1,0:T(8,128)S(1)}, u32[]{:S(2)}, u32[]{:S(2)}) collective-permute-start(f32[192,512]{1,0:T(8,128)S(1)} %collective-permute-done), channel_id=1, source_target_pairs={{0,16},{16,0},{1,17},{17,1},{2,18},{18,2},{3,19},{19,3},{4,20},{20... | collective-permute-start | bytes 1179656 | tf_op jit(solution)/shard_map/ppermute | solution.py:220
  32.9 30.1 %collective-permute-start.3 = (f32[384,512]{1,0:T(8,128)S(1)}, f32[384,512]{1,0:T(8,128)S(1)}, u32[]{:S(2)}, u32[]{:S(2)}) collective-permute-start(f32[384,512]{1,0:T(8,128)S(1)} %get-tuple-element.26), channel_id=1, source_target_pairs={{0,32},{32,64},{64,96},{96,0},{1,33},{33,65},{65,97},{97,1},{2,34}... | collective-permute-start | bytes 2359304 | tf_op jit(solution)/shard_map/ppermute | solution.py:222
  41.8 21.4 %collective-permute-start.2 = (f32[384,512]{1,0:T(8,128)S(1)}, f32[384,512]{1,0:T(8,128)S(1)}, u32[]{:S(2)}, u32[]{:S(2)}) collective-permute-start(f32[384,512]{1,0:T(8,128)S(1)} %get-tuple-element.26), channel_id=1, source_target_pairs={{0,96},{32,0},{64,32},{96,64},{1,97},{33,1},{65,33},{97,65},{2,98}... | collective-permute-start | bytes 2359304 | tf_op jit(solution)/shard_map/ppermute | solution.py:223
  63.0 10.1 %collective-permute-start.4 = (f32[192,512]{1,0:T(8,128)S(1)}, f32[192,512]{1,0:T(8,128)S(1)}, u32[]{:S(2)}, u32[]{:S(2)}) collective-permute-start(f32[192,512]{1,0:T(8,128)S(1)} %slice.88), channel_id=1, source_target_pairs={{0,32},{32,64},{64,96},{96,0},{1,33},{33,65},{65,97},{97,1},{2,34}... | collective-permute-start | bytes 1179656 | tf_op jit(solution)/shard_map/ppermute | solution.py:224
  63.2 10.0 %collective-permute-start.5 = (f32[192,512]{1,0:T(8,128)S(1)}, f32[192,512]{1,0:T(8,128)S(1)}, u32[]{:S(2)}, u32[]{:S(2)}) collective-permute-start(f32[192,512]{1,0:T(8,128)S(1)} %slice.89), channel_id=1, source_target_pairs={{0,96},{32,0},{64,32},{96,64},{1,97},{33,1},{65,33},{97,65},{2,98}... | collective-permute-start | bytes 1179656 | tf_op jit(solution)/shard_map/ppermute | solution.py:225
  73.3 23.2 %copy-start.3 = (f32[1,192,512]{2,1,0:T(8,128)S(1)}, f32[1,192,512]{2,1,0:T(8,128)}, u32[]{:S(2)}) copy-start(f32[1,192,512]{2,1,0:T(8,128)} %get-tuple-element.34) | copy-start | bytes 1179652
  83.0 46.0 %collective-permute-start.6 = (f32[8,192,512]{2,1,0:T(8,128)S(1)}, f32[8,192,512]{2,1,0:T(8,128)S(1)}, u32[]{:S(2)}, u32[]{:S(2)}) collective-permute-start(f32[8,192,512]{2,1,0:T(8,128)S(1)} %send_product.1), channel_id=1, source_target_pairs={{0,1},{1,0},{2,3},{3,2},{4,5},{5,4},{6,7},{7,6},{8,9},{9,8},{10,11... | collective-permute-start | bytes 9437192 | tf_op jit(solution)/shard_map/ppermute | solution.py:235
  85.9 10.6 %collective-permute-start.7 = (f32[192,512]{1,0:T(8,128)S(1)}, f32[192,512]{1,0:T(8,128)S(1)}, u32[]{:S(2)}, u32[]{:S(2)}) collective-permute-start(f32[192,512]{1,0:T(8,128)S(1)} %get-tuple-element.35.own_rows), channel_id=1, source_target_pairs={{0,8},{8,0},{1,9},{9,1},{2,10},{10,2},{3,11},{11,3},{4,12},{12,4},... | collective-permute-start | bytes 1179656 | tf_op jit(solution)/shard_map/ppermute | solution.py:227
  96.5 19.4 %collective-permute-start.9 = (f32[2,192,512]{2,1,0:T(8,128)S(1)}, f32[2,192,512]{2,1,0:T(8,128)S(1)}, u32[]{:S(2)}, u32[]{:S(2)}) collective-permute-start(f32[2,192,512]{2,1,0:T(8,128)S(1)} %pad_maximum_fusion), channel_id=1, source_target_pairs={{0,2},{2,4},{4,6},{6,0},{1,3},{3,5},{5,7},{7,1},{8,10},{10,12},{12... | collective-permute-start | bytes 2359304 | tf_op jit(solution)/shard_map/ppermute | solution.py:229
  99.7 18.5 %collective-permute-start.8 = (f32[2,192,512]{2,1,0:T(8,128)S(1)}, f32[2,192,512]{2,1,0:T(8,128)S(1)}, u32[]{:S(2)}, u32[]{:S(2)}) collective-permute-start(f32[2,192,512]{2,1,0:T(8,128)S(1)} %pad_maximum_fusion), channel_id=1, source_target_pairs={{0,6},{2,0},{4,2},{6,4},{1,7},{3,1},{5,3},{7,5},{8,14},{10,8},{12,... | collective-permute-start | bytes 2359304 | tf_op jit(solution)/shard_map/ppermute | solution.py:230
  116.0 13.1 %collective-permute-start.10 = (f32[192,512]{1,0:T(8,128)S(1)}, f32[192,512]{1,0:T(8,128)S(1)}, u32[]{:S(2)}, u32[]{:S(2)}) collective-permute-start(f32[192,512]{1,0:T(8,128)S(1)} %slice_bitcast_fusion.1), channel_id=1, source_target_pairs={{0,2},{2,4},{4,6},{6,0},{1,3},{3,5},{5,7},{7,1},{8,10},{10,12},{12... | collective-permute-start | bytes 1179656 | tf_op jit(solution)/shard_map/ppermute | solution.py:231
  118.2 10.8 %collective-permute-start.11 = (f32[192,512]{1,0:T(8,128)S(1)}, f32[192,512]{1,0:T(8,128)S(1)}, u32[]{:S(2)}, u32[]{:S(2)}) collective-permute-start(f32[192,512]{1,0:T(8,128)S(1)} %slice_bitcast_fusion), channel_id=1, source_target_pairs={{0,6},{2,0},{4,2},{6,4},{1,7},{3,1},{5,3},{7,5},{8,14},{10,8},{12,... | collective-permute-start | bytes 1179656 | tf_op jit(solution)/shard_map/ppermute | solution.py:232
  131.8 4.7 %collective-permute-start.17 = (f32[4,96,256]{2,1,0:T(8,128)S(1)}, f32[4,96,256]{2,1,0:T(8,128)S(1)}, u32[]{:S(2)}, u32[]{:S(2)}) collective-permute-start(f32[4,96,256]{2,1,0:T(8,128)S(1)} %slice_bitcast_fusion.2), channel_id=1, source_target_pairs={{0,1},{1,0},{2,3},{3,2},{4,5},{5,4},{6,7},{7,6},{8,9},{9,8},{10,11... | collective-permute-start | bytes 1179656 | tf_op jit(solution)/shard_map/ppermute | solution.py:206
  133.8 15.3 %collective-permute-start.12 = (f32[2,96,512]{2,1,0:T(8,128)S(1)}, f32[2,96,512]{2,1,0:T(8,128)S(1)}, u32[]{:S(2)}, u32[]{:S(2)}) collective-permute-start(f32[2,96,512]{2,1,0:T(8,128)S(1)} %get-tuple-element.16), channel_id=1, source_target_pairs={{0,2},{2,4},{4,6},{6,0},{1,3},{3,5},{5,7},{7,1},{8,10},{10,12},{12... | collective-permute-start | bytes 1179656 | tf_op jit(solution)/shard_map/ppermute | solution.py:240
  134.5 10.5 %collective-permute-start.14 = (f32[2,96,512]{2,1,0:T(8,128)S(1)}, f32[2,96,512]{2,1,0:T(8,128)S(1)}, u32[]{:S(2)}, u32[]{:S(2)}) collective-permute-start(f32[2,96,512]{2,1,0:T(8,128)S(1)} %get-tuple-element.18), channel_id=1, source_target_pairs={{0,6},{2,0},{4,2},{6,4},{1,7},{3,1},{5,3},{7,5},{8,14},{10,8},{12,... | collective-permute-start | bytes 1179656 | tf_op jit(solution)/shard_map/ppermute | solution.py:241
  136.6 13.2 %collective-permute-start.20 = (f32[96,256]{1,0:T(8,128)S(1)}, f32[96,256]{1,0:T(8,128)S(1)}, u32[]{:S(2)}, u32[]{:S(2)}) collective-permute-start(f32[96,256]{1,0:T(8,128)S(1)} %get-tuple-element.31), channel_id=1, source_target_pairs={{0,6},{2,4},{4,2},{6,0},{1,7},{3,5},{5,3},{7,1},{8,14},{10,12},{12... | collective-permute-start | bytes 294920 | tf_op jit(solution)/shard_map/ppermute | solution.py:207
  136.9 13.0 %collective-permute-start.19 = (f32[96,256]{1,0:T(8,128)S(1)}, f32[96,256]{1,0:T(8,128)S(1)}, u32[]{:S(2)}, u32[]{:S(2)}) collective-permute-start(f32[96,256]{1,0:T(8,128)S(1)} %get-tuple-element.32), channel_id=1, source_target_pairs={{0,4},{2,6},{4,0},{6,2},{1,5},{3,7},{5,1},{7,3},{8,12},{10,14},{12... | collective-permute-start | bytes 294920 | tf_op jit(solution)/shard_map/ppermute | solution.py:207
  138.1 11.8 %collective-permute-start.18 = (f32[96,256]{1,0:T(8,128)S(1)}, f32[96,256]{1,0:T(8,128)S(1)}, u32[]{:S(2)}, u32[]{:S(2)}) collective-permute-start(f32[96,256]{1,0:T(8,128)S(1)} %get-tuple-element.33), channel_id=1, source_target_pairs={{0,2},{2,0},{4,6},{6,4},{1,3},{3,1},{5,7},{7,5},{8,10},{10,8},{12,... | collective-permute-start | bytes 294920 | tf_op jit(solution)/shard_map/ppermute | solution.py:207
  145.1 33.9 %collective-permute-start.15 = (f32[2,192,512]{2,1,0:T(8,128)S(1)}, f32[2,192,512]{2,1,0:T(8,128)S(1)}, u32[]{:S(2)}, u32[]{:S(2)}) collective-permute-start(f32[2,192,512]{2,1,0:T(8,128)S(1)} %pad_maximum_fusion.2), channel_id=1, source_target_pairs={{0,6},{2,0},{4,2},{6,4},{1,7},{3,1},{5,3},{7,5},{8,14},{10,8},{12,... | collective-permute-start | bytes 2359304 | tf_op jit(solution)/shard_map/ppermute | solution.py:245
  149.2 31.2 %copy-start = (f32[256,256]{1,0:T(8,128)S(1)}, f32[256,256]{1,0:T(8,128)}, u32[]{:S(2)}) copy-start(f32[256,256]{1,0:T(8,128)} %child_top.1) | copy-start | bytes 786436
  149.2 31.2 %copy-start.1 = (f32[256,256]{1,0:T(8,128)S(1)}, f32[256,256]{1,0:T(8,128)}, u32[]{:S(2)}) copy-start(f32[256,256]{1,0:T(8,128)} %diag_parent.1) | copy-start | bytes 786436
  149.2 31.2 %copy-start.2 = (f32[256,256]{1,0:T(8,128)S(1)}, f32[256,256]{1,0:T(8,128)}, u32[]{:S(2)}) copy-start(f32[256,256]{1,0:T(8,128)} %diag_child.1) | copy-start | bytes 786436
  149.9 5.4 %collective-permute-start.23 = (f32[96,256]{1,0:T(8,128)S(1)}, f32[96,256]{1,0:T(8,128)S(1)}, u32[]{:S(2)}, u32[]{:S(2)}) collective-permute-start(f32[96,256]{1,0:T(8,128)S(1)} %fusion.7), channel_id=1, source_target_pairs={{0,96},{32,64},{64,32},{96,0},{1,97},{33,65},{65,33},{97,1},{2,98}... | collective-permute-start | bytes 294920 | tf_op jit(solution)/shard_map/ppermute | solution.py:209
  152.7 5.0 %collective-permute-start.22 = (f32[96,256]{1,0:T(8,128)S(1)}, f32[96,256]{1,0:T(8,128)S(1)}, u32[]{:S(2)}, u32[]{:S(2)}) collective-permute-start(f32[96,256]{1,0:T(8,128)S(1)} %fusion.7), channel_id=1, source_target_pairs={{0,64},{32,96},{64,0},{96,32},{1,65},{33,97},{65,1},{97,33},{2,66}... | collective-permute-start | bytes 294920 | tf_op jit(solution)/shard_map/ppermute | solution.py:209
  152.7 5.0 %collective-permute-start.21 = (f32[96,256]{1,0:T(8,128)S(1)}, f32[96,256]{1,0:T(8,128)S(1)}, u32[]{:S(2)}, u32[]{:S(2)}) collective-permute-start(f32[96,256]{1,0:T(8,128)S(1)} %fusion.7), channel_id=1, source_target_pairs={{0,32},{32,0},{64,96},{96,64},{1,33},{33,1},{65,97},{97,65},{2,34}... | collective-permute-start | bytes 294920 | tf_op jit(solution)/shard_map/ppermute | solution.py:209
  153.4 25.6 %collective-permute-start.13 = (f32[2,192,512]{2,1,0:T(8,128)S(1)}, f32[2,192,512]{2,1,0:T(8,128)S(1)}, u32[]{:S(2)}, u32[]{:S(2)}) collective-permute-start(f32[2,192,512]{2,1,0:T(8,128)S(1)} %pad_maximum_fusion.1), channel_id=1, source_target_pairs={{0,2},{2,4},{4,6},{6,0},{1,3},{3,5},{5,7},{7,1},{8,10},{10,12},{12... | collective-permute-start | bytes 2359304 | tf_op jit(solution)/shard_map/ppermute | solution.py:244
  157.8 5.1 %collective-permute-start.26 = (f32[96,256]{1,0:T(8,128)S(1)}, f32[96,256]{1,0:T(8,128)S(1)}, u32[]{:S(2)}, u32[]{:S(2)}) collective-permute-start(f32[96,256]{1,0:T(8,128)S(1)} %add_add_fusion.1), channel_id=1, source_target_pairs={{0,24},{8,16},{16,8},{24,0},{1,25},{9,17},{17,9},{25,1},{2,26},{10... | collective-permute-start | bytes 294920 | tf_op jit(solution)/shard_map/ppermute | solution.py:211
  159.9 5.0 %collective-permute-start.25 = (f32[96,256]{1,0:T(8,128)S(1)}, f32[96,256]{1,0:T(8,128)S(1)}, u32[]{:S(2)}, u32[]{:S(2)}) collective-permute-start(f32[96,256]{1,0:T(8,128)S(1)} %add_add_fusion.1), channel_id=1, source_target_pairs={{0,16},{8,24},{16,0},{24,8},{1,17},{9,25},{17,1},{25,9},{2,18},{10... | collective-permute-start | bytes 294920 | tf_op jit(solution)/shard_map/ppermute | solution.py:211
  160.8 4.0 %collective-permute-start.24 = (f32[96,256]{1,0:T(8,128)S(1)}, f32[96,256]{1,0:T(8,128)S(1)}, u32[]{:S(2)}, u32[]{:S(2)}) collective-permute-start(f32[96,256]{1,0:T(8,128)S(1)} %add_add_fusion.1), channel_id=1, source_target_pairs={{0,8},{8,0},{16,24},{24,16},{1,9},{9,1},{17,25},{25,17},{2,10},{10... | collective-permute-start | bytes 294920 | tf_op jit(solution)/shard_map/ppermute | solution.py:211
  164.9 7.4 %collective-permute-start.29 = (f32[96,256]{1,0:T(8,128)S(1)}, f32[96,256]{1,0:T(8,128)S(1)}, u32[]{:S(2)}, u32[]{:S(2)}) collective-permute-start(f32[96,256]{1,0:T(8,128)S(1)} %add_add_fusion), channel_id=1, source_target_pairs={{0,6},{2,4},{4,2},{6,0},{1,7},{3,5},{5,3},{7,1},{8,14},{10,12},{12... | collective-permute-start | bytes 294920 | tf_op jit(solution)/shard_map/ppermute | solution.py:213
  167.0 7.5 %collective-permute-start.28 = (f32[96,256]{1,0:T(8,128)S(1)}, f32[96,256]{1,0:T(8,128)S(1)}, u32[]{:S(2)}, u32[]{:S(2)}) collective-permute-start(f32[96,256]{1,0:T(8,128)S(1)} %add_add_fusion), channel_id=1, source_target_pairs={{0,4},{2,6},{4,0},{6,2},{1,5},{3,7},{5,1},{7,3},{8,12},{10,14},{12... | collective-permute-start | bytes 294920 | tf_op jit(solution)/shard_map/ppermute | solution.py:213
  167.0 7.5 %collective-permute-start.27 = (f32[96,256]{1,0:T(8,128)S(1)}, f32[96,256]{1,0:T(8,128)S(1)}, u32[]{:S(2)}, u32[]{:S(2)}) collective-permute-start(f32[96,256]{1,0:T(8,128)S(1)} %add_add_fusion), channel_id=1, source_target_pairs={{0,2},{2,0},{4,6},{6,4},{1,3},{3,1},{5,7},{7,5},{8,10},{10,8},{12,... | collective-permute-start | bytes 294920 | tf_op jit(solution)/shard_map/ppermute | solution.py:213
  174.6 5.8 %collective-permute-start.30 = (f32[4,96,256]{2,1,0:T(8,128)S(1)}, f32[4,96,256]{2,1,0:T(8,128)S(1)}, u32[]{:S(2)}, u32[]{:S(2)}) collective-permute-start(f32[4,96,256]{2,1,0:T(8,128)S(1)} %pad_maximum_fusion.4.own), channel_id=1, source_target_pairs={{0,1},{1,0},{2,3},{3,2},{4,5},{5,4},{6,7},{7,6},{8,9},{9,8},{10,11... | collective-permute-start | bytes 1179656 | tf_op jit(solution)/shard_map/ppermute | solution.py:214
  179.1 10.7 %collective-permute-start.16 = (f32[192,512]{1,0:T(8,128)S(1)}, f32[192,512]{1,0:T(8,128)S(1)}, u32[]{:S(2)}, u32[]{:S(2)}) collective-permute-start(f32[192,512]{1,0:T(8,128)S(1)} %fusion.2), channel_id=1, source_target_pairs={{0,8},{8,0},{1,9},{9,1},{2,10},{10,2},{3,11},{11,3},{4,12},{12,4},... | collective-permute-start | bytes 1179656 | tf_op jit(solution)/shard_map/ppermute | solution.py:246
  190.1 1.0 copy-start.4
